TPU v7x, 32 devices: a whole 2x2x4 slice. The times are simulated.
32 devices in a mesh: depth: 8 (over z, core), image: 4 (over y, x).
Axes of the slice: x: 2, y: 2, z: 4, core: 2. Of those that a mesh axis runs over, the one named last changes fastest.
Arguments:
- level_set: float32 [128, 256, 512], P('depth', 'image'), may hold values from -6 to 6
- velocity: float32 [3, 128, 256, 512], P(None, 'depth', 'image'), may hold values from -1 to 1
- view_flag: int32 [8], replicated, may hold values from 0 to 1
- slab_rank: int32 [8], replicated, may hold values from 0 to 7, each once
Outputs:
- image_first: float32 [4, 256, 512], P(None, 'image', 'depth')
- image_second: float32 [4, 256, 512], P(None, 'image', 'depth')
- level_next: float32 [128, 256, 512], P('depth', 'image')
Inputs may be any that keep to these rules, and one draw needn't show every extreme that they name: `slab_rank`: each of 0 to 7 once.
All inputs are finite; a program needn't handle non-finite values.
Results may differ from a plain program's by a relative error of at most 0.00013.
Values sent between devices are 32-bit elements; how exact they have to be, the bound alone decides.
No kernel may reach another device: no remote copies, remote signals or barrier semaphores. Data moves between devices by JAX's collectives and lax.ppermute only.
A program may use at most 64 MiB of HBM per device.

v0:
```python
import jax
import jax.numpy as jnp
from jax import lax
from jax.sharding import PartitionSpec as P

STEPS = 4


step_size = 0.3


def extended(block, sides, width):
    for axis, dim in sides:
        count = lax.axis_size(axis)
        forward = [(i, i + 1) for i in range(count - 1)]
        backward = [(target, source) for source, target in forward]
        low = lax.ppermute(
            lax.slice_in_dim(block, block.shape[dim] - width, None, axis=dim), axis, forward
        )
        high = lax.ppermute(lax.slice_in_dim(block, 0, width, axis=dim), axis, backward)
        block = jnp.concatenate([low, block, high], axis=dim)
    return block


def update(padded, velocity):
    center = padded[1:-1, 1:-1, 1:-1]
    lows = (padded[:-2, 1:-1, 1:-1], padded[1:-1, :-2, 1:-1], padded[1:-1, 1:-1, :-2])
    highs = (padded[2:, 1:-1, 1:-1], padded[1:-1, 2:, 1:-1], padded[1:-1, 1:-1, 2:])
    rate = jnp.zeros_like(center)
    for k in range(3):
        speed = velocity[k]
        rate = (
            rate
            + jnp.maximum(speed, 0.0) * (center - lows[k])
            + jnp.minimum(speed, 0.0) * (highs[k] - center)
        )
    return center - step_size * rate


def advect_single(field, velocity):
    padded = extended(field, (("depth", 0), ("image", 1)), 1)
    padded = jnp.pad(padded, ((0, 0), (0, 0), (1, 1)))
    return update(padded, velocity)


def render_brick(field, flag, scale):
    density = scale * jnp.exp(-field * field)
    colour = jnp.stack(
        [jax.nn.sigmoid(2.0 * field), jnp.exp(-field * field), jax.nn.sigmoid(-2.0 * field)], axis=0
    )
    running = jnp.cumsum(density, axis=0)
    totals = running[-1:]
    before = jnp.where(flag[0] == 0, running - density, totals - running)
    weight = jnp.exp(-before) * (1.0 - jnp.exp(-density))
    partial_colour = jnp.sum(weight[None] * colour, axis=1)
    return (partial_colour, -totals[0])


def composite(frames, slab_rank):
    count = len(frames)
    depth_count = lax.axis_size("depth")
    colours = jnp.stack([frame[0] for frame in frames], axis=0)
    logs = jnp.stack([frame[1] for frame in frames], axis=0)
    rows, cols = (logs.shape[1], logs.shape[2])
    width = cols // depth_count
    packed = jnp.concatenate([colours, logs[:, None]], axis=1)
    received = lax.all_to_all(packed, "depth", split_axis=3, concat_axis=0, tiled=True)
    received = received.reshape(depth_count, count, 4, rows, width)
    earlier_mask = (slab_rank[None, :] < slab_rank[:, None]).astype(jnp.float32)
    log_parts = received[:, :, 3]
    earlier = jnp.einsum("de,efxy->dfxy", earlier_mask, log_parts, precision=lax.Precision.HIGHEST)
    rgb = jnp.sum(jnp.exp(earlier)[:, :, None] * received[:, :, :3], axis=0)
    alpha = 1.0 - jnp.exp(jnp.sum(log_parts, axis=0))
    result = jnp.concatenate([rgb, alpha[:, None]], axis=1)
    return [result[0]]


def local(level_set, velocity, view_flag, slab_rank):
    scale = 2.0 / (level_set.shape[0] * lax.axis_size("depth"))
    own_flag = lax.dynamic_slice_in_dim(view_flag, lax.axis_index("depth"), 1)
    first = render_brick(level_set, own_flag, scale)
    field = level_set
    for step in range(STEPS):
        field = advect_single(field, velocity)
    second = render_brick(field, own_flag, scale)
    image_first = composite([first], slab_rank)[0]
    image_second = composite([second], slab_rank)[0]
    return (image_first, image_second, field)


def solution(mesh):
    placed = (P("depth", "image", None), P(None, "depth", "image", None), P(), P())
    return jax.shard_map(
        local,
        mesh=mesh,
        in_specs=placed,
        out_specs=(P(None, "image", "depth"), P(None, "image", "depth"), P("depth", "image", None)),
        check_vma=False,
    )
```

profile of v0, /device:TPU:4, one launch (start us, length us, event | category | flops | bytes accessed | tf_op | source)
XLA Modules:
  0.0 144.6 jit_solution(2762849971171478497)
XLA Ops:
  4.8 2.0 %fusion.75 = f32[16,64,512]{2,1,0:T(8,128)S(1)} fusion(f32[16,64,512]{2,1,0:T(8,128)} %param.4), kind=kOutput, calls=%fused_computation.143 | output fusion | flops 9437184 | bytes 4194304 | tf_op jit(solution)/shard_map/jit(cumsum)/reduce_window_sum | solution.py:51
  9.6 3.3 %collective-permute-start.3 = (f32[18,1,512]{2,1,0:T(1,128)S(1)}, f32[18,1,512]{2,1,0:T(1,128)S(1)}, u32[]{:S(2)}, u32[]{:S(2)}) collective-permute-start(f32[18,1,512]{2,1,0:T(1,128)S(1)} %get-tuple-element.12), channel_id=1, source_target_pairs={{1,0},{2,1},{3,2},{5,4},{6,5},{7,6},{9,8},{10,9},{11,10},{13,12},{... | collective-permute-start | bytes 110600 | tf_op jit(solution)/shard_map/ppermute | solution.py:20
  13.0 2.5 %collective-permute-start.2 = (f32[18,1,512]{2,1,0:T(1,128)S(1)}, f32[18,1,512]{2,1,0:T(1,128)S(1)}, u32[]{:S(2)}, u32[]{:S(2)}) collective-permute-start(f32[18,1,512]{2,1,0:T(1,128)S(1)} %get-tuple-element.11), channel_id=1, source_target_pairs={{0,1},{1,2},{2,3},{4,5},{5,6},{6,7},{8,9},{9,10},{10,11},{12,13},{... | collective-permute-start | bytes 110600 | tf_op jit(solution)/shard_map/ppermute | solution.py:17
  16.8 2.9 %collective-permute-done.2 = f32[18,1,512]{2,1,0:T(1,128)S(1)} collective-permute-done((f32[18,1,512]{2,1,0:T(1,128)S(1)}, f32[18,1,512]{2,1,0:T(1,128)S(1)}, u32[]{:S(2)}, u32[]{:S(2)}) %collective-permute-start.2) | collective-permute-done | bytes 36896 | tf_op jit(solution)/shard_map/ppermute | solution.py:17
  19.7 3.1 %select_maximum_fusion.12 = f32[18,66,514]{2,1,0:T(8,128)S(1)} fusion(f32[18,1,512]{2,1,0:T(1,128)S(1)} %collective-permute-done.3, f32[18,64,512]{2,1,0:T(8,128)} %copy-done.2, f32[18,1,512]{2,1,0:T(1,128)S(1)} %collective-permute-done.2), kind=kLoop, calls=%fused_computation.18 | loop fusion | flops 4885056 | bytes 4875552 | tf_op jit(solution)/shard_map/concatenate | solution.py:21
  22.9 10.2 %fusion.59 = (f32[16,64,512]{2,1,0:T(8,128)S(1)}, f32[1,16,64,512]{3,2,1,0:T(8,128)}, f32[16,64,512]{2,1,0:T(8,128)}, f32[1,16,64,512]{3,2,1,0:T(8,128)}, f32[1,16,64,512]{3,2,1,0:T(8,128)}) fusion(f32[16,64,512]{2,1,0:T(8,128)S(1)} %copy-done, f32[18,66,514]{2,1,0:T(8,128)S(1)} %select_maximum_fusion.12, f32[18,1,512]{2,1,0:T(1,128)S(1)} %collective-permute-done.3, ...), kind=kLoop, calls=%fused_computation.110 | loop fusion | flops 24641536 | bytes 27992064 | tf_op jit(solution)/shard_map/sub | solution.py:37
  34.4 4.7 %collective-permute-start.4 = (f32[1,64,512]{2,1,0:T(8,128)S(1)}, f32[1,64,512]{2,1,0:T(8,128)S(1)}, u32[]{:S(2)}, u32[]{:S(2)}) collective-permute-start(f32[1,64,512]{2,1,0:T(8,128)S(1)} %get-tuple-element.22), channel_id=1, source_target_pairs={{0,4},{4,8},{8,12},{12,16},{16,20},{20,24},{24,28},{1,5},{5,9},{9,... | collective-permute-start | bytes 393224 | tf_op jit(solution)/shard_map/ppermute | solution.py:17
  40.1 2.2 %collective-permute-start.7 = (f32[18,1,512]{2,1,0:T(1,128)S(1)}, f32[18,1,512]{2,1,0:T(1,128)S(1)}, u32[]{:S(2)}, u32[]{:S(2)}) collective-permute-start(f32[18,1,512]{2,1,0:T(1,128)S(1)} %get-tuple-element.10), channel_id=1, source_target_pairs={{1,0},{2,1},{3,2},{5,4},{6,5},{7,6},{9,8},{10,9},{11,10},{13,12},{... | collective-permute-start | bytes 110600 | tf_op jit(solution)/shard_map/ppermute | solution.py:20
  42.3 3.6 %collective-permute-start.6 = (f32[18,1,512]{2,1,0:T(1,128)S(1)}, f32[18,1,512]{2,1,0:T(1,128)S(1)}, u32[]{:S(2)}, u32[]{:S(2)}) collective-permute-start(f32[18,1,512]{2,1,0:T(1,128)S(1)} %get-tuple-element.9), channel_id=1, source_target_pairs={{0,1},{1,2},{2,3},{4,5},{5,6},{6,7},{8,9},{9,10},{10,11},{12,13},{... | collective-permute-start | bytes 110600 | tf_op jit(solution)/shard_map/ppermute | solution.py:17
  46.0 3.1 %collective-permute-done.6 = f32[18,1,512]{2,1,0:T(1,128)S(1)} collective-permute-done((f32[18,1,512]{2,1,0:T(1,128)S(1)}, f32[18,1,512]{2,1,0:T(1,128)S(1)}, u32[]{:S(2)}, u32[]{:S(2)}) %collective-permute-start.6) | collective-permute-done | bytes 36896 | tf_op jit(solution)/shard_map/ppermute | solution.py:17
  49.1 3.0 %select_maximum_fusion.8 = f32[18,66,514]{2,1,0:T(8,128)S(1)} fusion(f32[18,1,512]{2,1,0:T(1,128)S(1)} %collective-permute-done.7, f32[18,1,512]{2,1,0:T(1,128)S(1)} %collective-permute-done.6, f32[1,64,512]{2,1,0:T(8,128)S(1)} %collective-permute-done.5, f32[16,64,512]{2,1,0:T(8,128)S(1)} %get-tuple-element.24, f32[1,64,512]{2,1,0:T(8,128)S(1)} %collective-permute-done.4), kind=kLoop, calls=%fused_computation.14 | loop fusion | flops 7327584 | bytes 4875552 | tf_op jit(solution)/shard_map/concatenate | solution.py:21
  52.1 3.3 %fusion.42 = f32[16,64,512]{2,1,0:T(8,128)S(1)} fusion(f32[16,64,512]{2,1,0:T(8,128)S(1)} %get-tuple-element.24, f32[18,66,514]{2,1,0:T(8,128)S(1)} %select_maximum_fusion.8, f32[18,1,512]{2,1,0:T(1,128)S(1)} %collective-permute-done.7, f32[1,64,512]{2,1,0:T(8,128)S(1)} %collective-permute-done.5, f32[1,64,512]{2,1,0:T(8,128)S(1)} %collective-permute-done.4, ...), kind=kLoop, calls=%fused_computation.83 | loop fusion | flops 17301504 | bytes 15015936 | tf_op jit(solution)/shard_map/sub | solution.py:37
  56.7 3.8 %collective-permute-start.8 = (f32[1,64,512]{2,1,0:T(8,128)S(1)}, f32[1,64,512]{2,1,0:T(8,128)S(1)}, u32[]{:S(2)}, u32[]{:S(2)}) collective-permute-start(f32[1,64,512]{2,1,0:T(8,128)S(1)} %get-tuple-element.20), channel_id=1, source_target_pairs={{0,4},{4,8},{8,12},{12,16},{16,20},{20,24},{24,28},{1,5},{5,9},{9,... | collective-permute-start | bytes 393224 | tf_op jit(solution)/shard_map/ppermute | solution.py:17
  63.5 4.1 %collective-permute-start.10 = (f32[18,1,512]{2,1,0:T(1,128)S(1)}, f32[18,1,512]{2,1,0:T(1,128)S(1)}, u32[]{:S(2)}, u32[]{:S(2)}) collective-permute-start(f32[18,1,512]{2,1,0:T(1,128)S(1)} %get-tuple-element.7), channel_id=1, source_target_pairs={{0,1},{1,2},{2,3},{4,5},{5,6},{6,7},{8,9},{9,10},{10,11},{12,13},{... | collective-permute-start | bytes 110600 | tf_op jit(solution)/shard_map/ppermute | solution.py:17
  67.6 2.6 %collective-permute-done.10 = f32[18,1,512]{2,1,0:T(1,128)S(1)} collective-permute-done((f32[18,1,512]{2,1,0:T(1,128)S(1)}, f32[18,1,512]{2,1,0:T(1,128)S(1)}, u32[]{:S(2)}, u32[]{:S(2)}) %collective-permute-start.10) | collective-permute-done | bytes 36896 | tf_op jit(solution)/shard_map/ppermute | solution.py:17
  70.2 3.0 %select_maximum_fusion.4 = f32[18,66,514]{2,1,0:T(8,128)S(1)} fusion(f32[18,1,512]{2,1,0:T(1,128)S(1)} %collective-permute-done.11, f32[18,1,512]{2,1,0:T(1,128)S(1)} %collective-permute-done.10, f32[1,64,512]{2,1,0:T(8,128)S(1)} %collective-permute-done.9, f32[16,64,512]{2,1,0:T(8,128)S(1)} %fusion.42, f32[1,64,512]{2,1,0:T(8,128)S(1)} %collective-permute-done.8), kind=kLoop, calls=%fused_computation.10 | loop fusion | flops 7327584 | bytes 4875552 | tf_op jit(solution)/shard_map/concatenate | solution.py:21
  73.3 3.3 %fusion.25 = f32[16,64,512]{2,1,0:T(8,128)S(1)} fusion(f32[16,64,512]{2,1,0:T(8,128)S(1)} %fusion.42, f32[18,66,514]{2,1,0:T(8,128)S(1)} %select_maximum_fusion.4, f32[18,1,512]{2,1,0:T(1,128)S(1)} %collective-permute-done.11, f32[1,64,512]{2,1,0:T(8,128)S(1)} %collective-permute-done.9, f32[1,64,512]{2,1,0:T(8,128)S(1)} %collective-permute-done.8, ...), kind=kLoop, calls=%fused_computation.56 | loop fusion | flops 17301504 | bytes 15015936 | tf_op jit(solution)/shard_map/sub | solution.py:37
  77.9 6.2 %collective-permute-start.12 = (f32[1,64,512]{2,1,0:T(8,128)S(1)}, f32[1,64,512]{2,1,0:T(8,128)S(1)}, u32[]{:S(2)}, u32[]{:S(2)}) collective-permute-start(f32[1,64,512]{2,1,0:T(8,128)S(1)} %get-tuple-element.18), channel_id=1, source_target_pairs={{0,4},{4,8},{8,12},{12,16},{16,20},{20,24},{24,28},{1,5},{5,9},{9,... | collective-permute-start | bytes 393224 | tf_op jit(solution)/shard_map/ppermute | solution.py:17
  87.3 3.9 %collective-permute-start.14 = (f32[18,1,512]{2,1,0:T(1,128)S(1)}, f32[18,1,512]{2,1,0:T(1,128)S(1)}, u32[]{:S(2)}, u32[]{:S(2)}) collective-permute-start(f32[18,1,512]{2,1,0:T(1,128)S(1)} %get-tuple-element.5), channel_id=1, source_target_pairs={{0,1},{1,2},{2,3},{4,5},{5,6},{6,7},{8,9},{9,10},{10,11},{12,13},{... | collective-permute-start | bytes 110600 | tf_op jit(solution)/shard_map/ppermute | solution.py:17
  95.3 10.0 %all-to-all-start = ((f32[8,1,16384]{2,1,0:T(1,128)}), f32[8,1,16384]{2,1,0:T(1,128)S(1)}, u32[]{:S(2)}, u32[]{:S(2)}) async-start(f32[8,1,16384]{2,1,0:T(1,128)} %reshape.111), calls=%async_computation | async-start | bytes 1048576 | tf_op jit(solution)/shard_map/all_to_all | solution.py:67
  105.3 3.0 %select_maximum_fusion = f32[18,66,514]{2,1,0:T(8,128)S(1)} fusion(f32[18,1,512]{2,1,0:T(1,128)S(1)} %collective-permute-done.15, f32[18,1,512]{2,1,0:T(1,128)S(1)} %collective-permute-done.14, f32[1,64,512]{2,1,0:T(8,128)S(1)} %collective-permute-done.13, f32[16,64,512]{2,1,0:T(8,128)S(1)} %fusion.25, f32[1,64,512]{2,1,0:T(8,128)S(1)} %collective-permute-done.12), kind=kLoop, calls=%fused_computation.6 | loop fusion | flops 7327584 | bytes 4875552 | tf_op jit(solution)/shard_map/concatenate | solution.py:21
  108.3 5.5 %divide_bitcast_fusion.1 = (f32[1,16,64,512]{3,2,1,0:T(8,128)S(1)}, f32[16,64,512]{2,1,0:T(8,128)S(1)}) fusion(f32[16,64,512]{2,1,0:T(8,128)S(1)} %fusion.25, f32[18,66,514]{2,1,0:T(8,128)S(1)} %select_maximum_fusion, f32[3,16,64,512]{3,2,1,0:T(8,128)} %param.5, f32[18,1,512]{2,1,0:T(1,128)S(1)} %collective-permute-done.15, ...), kind=kLoop, calls=%fused_computation.130 | loop fusion | flops 19398656 | bytes 17113088 | tf_op jit(solution)/shard_map/stack | solution.py:48
  120.6 4.3 %all-to-all-start.1 = ((f32[8,1,16384]{2,1,0:T(1,128)}), f32[8,1,16384]{2,1,0:T(1,128)S(1)}, u32[]{:S(2)}, u32[]{:S(2)}) async-start(f32[8,1,16384]{2,1,0:T(1,128)} %reshape.113), calls=%async_computation.1 | async-start | bytes 1048576 | tf_op jit(solution)/shard_map/all_to_all | solution.py:67
  129.8 10.4 %all-to-all-done.1 = f32[8,1,16384]{2,1,0:T(1,128)S(1)} async-done(((f32[8,1,16384]{2,1,0:T(1,128)}), f32[8,1,16384]{2,1,0:T(1,128)S(1)}, u32[]{:S(2)}, u32[]{:S(2)}) %all-to-all-start.1) | async-done | bytes 524320 | tf_op jit(solution)/shard_map/all_to_all | solution.py:67
  (91 shorter events, 38.4 us)
Async XLA Ops:
  1.6 5.2 %collective-permute-start = (f32[1,64,512]{2,1,0:T(8,128)S(1)}, f32[1,64,512]{2,1,0:T(8,128)S(1)}, u32[]{:S(2)}, u32[]{:S(2)}) collective-permute-start(f32[1,64,512]{2,1,0:T(8,128)S(1)} %get-tuple-element.30), channel_id=1, source_target_pairs={{0,4},{4,8},{8,12},{12,16},{16,20},{20,24},{24,28},{1,5},{5,9},{9,... | collective-permute-start | bytes 393224 | tf_op jit(solution)/shard_map/ppermute | solution.py:17
  3.4 4.7 %collective-permute-start.1 = (f32[1,64,512]{2,1,0:T(8,128)S(1)}, f32[1,64,512]{2,1,0:T(8,128)S(1)}, u32[]{:S(2)}, u32[]{:S(2)}) collective-permute-start(f32[1,64,512]{2,1,0:T(8,128)S(1)} %get-tuple-element.29), channel_id=1, source_target_pairs={{4,0},{8,4},{12,8},{16,12},{20,16},{24,20},{28,24},{5,1},{9,5},{13... | collective-permute-start | bytes 393224 | tf_op jit(solution)/shard_map/ppermute | solution.py:20
  9.6 7.2 %collective-permute-start.3 = (f32[18,1,512]{2,1,0:T(1,128)S(1)}, f32[18,1,512]{2,1,0:T(1,128)S(1)}, u32[]{:S(2)}, u32[]{:S(2)}) collective-permute-start(f32[18,1,512]{2,1,0:T(1,128)S(1)} %get-tuple-element.12), channel_id=1, source_target_pairs={{1,0},{2,1},{3,2},{5,4},{6,5},{7,6},{9,8},{10,9},{11,10},{13,12},{... | collective-permute-start | bytes 110600 | tf_op jit(solution)/shard_map/ppermute | solution.py:20
  13.0 6.8 %collective-permute-start.2 = (f32[18,1,512]{2,1,0:T(1,128)S(1)}, f32[18,1,512]{2,1,0:T(1,128)S(1)}, u32[]{:S(2)}, u32[]{:S(2)}) collective-permute-start(f32[18,1,512]{2,1,0:T(1,128)S(1)} %get-tuple-element.11), channel_id=1, source_target_pairs={{0,1},{1,2},{2,3},{4,5},{5,6},{6,7},{8,9},{9,10},{10,11},{12,13},{... | collective-permute-start | bytes 110600 | tf_op jit(solution)/shard_map/ppermute | solution.py:17
  19.7 32.4 %slice-start = ((s8[6291456]{0:T(1024)(128)(4,1)}), s8[4194304]{0:T(1024)(128)(4,1)S(1)}, s32[]{:S(2)}) async-start(s8[6291456]{0:T(1024)(128)(4,1)} %bitcast.88), calls=%async_computation.2 | async-start | bytes 8388608
  22.9 29.2 %slice-start.1 = ((s8[6291456]{0:T(1024)(128)(4,1)}), s8[2097152]{0:T(1024)(128)(4,1)S(1)}, s32[]{:S(2)}) async-start(s8[6291456]{0:T(1024)(128)(4,1)} %bitcast.88), calls=%async_computation.3 | async-start | bytes 4194304
  33.1 6.0 %collective-permute-start.5 = (f32[1,64,512]{2,1,0:T(8,128)S(1)}, f32[1,64,512]{2,1,0:T(8,128)S(1)}, u32[]{:S(2)}, u32[]{:S(2)}) collective-permute-start(f32[1,64,512]{2,1,0:T(8,128)S(1)} %get-tuple-element.23), channel_id=1, source_target_pairs={{4,0},{8,4},{12,8},{16,12},{20,16},{24,20},{28,24},{5,1},{9,5},{13... | collective-permute-start | bytes 393224 | tf_op jit(solution)/shard_map/ppermute | solution.py:20
  34.4 5.6 %collective-permute-start.4 = (f32[1,64,512]{2,1,0:T(8,128)S(1)}, f32[1,64,512]{2,1,0:T(8,128)S(1)}, u32[]{:S(2)}, u32[]{:S(2)}) collective-permute-start(f32[1,64,512]{2,1,0:T(8,128)S(1)} %get-tuple-element.22), channel_id=1, source_target_pairs={{0,4},{4,8},{8,12},{12,16},{16,20},{20,24},{24,28},{1,5},{5,9},{9,... | collective-permute-start | bytes 393224 | tf_op jit(solution)/shard_map/ppermute | solution.py:17
  40.1 5.9 %collective-permute-start.7 = (f32[18,1,512]{2,1,0:T(1,128)S(1)}, f32[18,1,512]{2,1,0:T(1,128)S(1)}, u32[]{:S(2)}, u32[]{:S(2)}) collective-permute-start(f32[18,1,512]{2,1,0:T(1,128)S(1)} %get-tuple-element.10), channel_id=1, source_target_pairs={{1,0},{2,1},{3,2},{5,4},{6,5},{7,6},{9,8},{10,9},{11,10},{13,12},{... | collective-permute-start | bytes 110600 | tf_op jit(solution)/shard_map/ppermute | solution.py:20
  42.3 6.8 %collective-permute-start.6 = (f32[18,1,512]{2,1,0:T(1,128)S(1)}, f32[18,1,512]{2,1,0:T(1,128)S(1)}, u32[]{:S(2)}, u32[]{:S(2)}) collective-permute-start(f32[18,1,512]{2,1,0:T(1,128)S(1)} %get-tuple-element.9), channel_id=1, source_target_pairs={{0,1},{1,2},{2,3},{4,5},{5,6},{6,7},{8,9},{9,10},{10,11},{12,13},{... | collective-permute-start | bytes 110600 | tf_op jit(solution)/shard_map/ppermute | solution.py:17
  55.4 5.1 %collective-permute-start.9 = (f32[1,64,512]{2,1,0:T(8,128)S(1)}, f32[1,64,512]{2,1,0:T(8,128)S(1)}, u32[]{:S(2)}, u32[]{:S(2)}) collective-permute-start(f32[1,64,512]{2,1,0:T(8,128)S(1)} %get-tuple-element.21), channel_id=1, source_target_pairs={{4,0},{8,4},{12,8},{16,12},{20,16},{24,20},{28,24},{5,1},{9,5},{13... | collective-permute-start | bytes 393224 | tf_op jit(solution)/shard_map/ppermute | solution.py:20
  56.7 4.8 %collective-permute-start.8 = (f32[1,64,512]{2,1,0:T(8,128)S(1)}, f32[1,64,512]{2,1,0:T(8,128)S(1)}, u32[]{:S(2)}, u32[]{:S(2)}) collective-permute-start(f32[1,64,512]{2,1,0:T(8,128)S(1)} %get-tuple-element.20), channel_id=1, source_target_pairs={{0,4},{4,8},{8,12},{12,16},{16,20},{20,24},{24,28},{1,5},{5,9},{9,... | collective-permute-start | bytes 393224 | tf_op jit(solution)/shard_map/ppermute | solution.py:17
  61.6 6.0 %collective-permute-start.11 = (f32[18,1,512]{2,1,0:T(1,128)S(1)}, f32[18,1,512]{2,1,0:T(1,128)S(1)}, u32[]{:S(2)}, u32[]{:S(2)}) collective-permute-start(f32[18,1,512]{2,1,0:T(1,128)S(1)} %get-tuple-element.8), channel_id=1, source_target_pairs={{1,0},{2,1},{3,2},{5,4},{6,5},{7,6},{9,8},{10,9},{11,10},{13,12},{... | collective-permute-start | bytes 110600 | tf_op jit(solution)/shard_map/ppermute | solution.py:20
  63.5 6.8 %collective-permute-start.10 = (f32[18,1,512]{2,1,0:T(1,128)S(1)}, f32[18,1,512]{2,1,0:T(1,128)S(1)}, u32[]{:S(2)}, u32[]{:S(2)}) collective-permute-start(f32[18,1,512]{2,1,0:T(1,128)S(1)} %get-tuple-element.7), channel_id=1, source_target_pairs={{0,1},{1,2},{2,3},{4,5},{5,6},{6,7},{8,9},{9,10},{10,11},{12,13},{... | collective-permute-start | bytes 110600 | tf_op jit(solution)/shard_map/ppermute | solution.py:17
  73.2 11.0 %copy-start.6 = (f32[1,16,64,512]{3,2,1,0:T(8,128)S(1)}, f32[1,16,64,512]{3,2,1,0:T(8,128)}, u32[]{:S(2)}) copy-start(f32[1,16,64,512]{3,2,1,0:T(8,128)} %get-tuple-element.25) | copy-start | bytes 6291460
  73.2 11.0 %copy-start.7 = (f32[16,64,512]{2,1,0:T(8,128)S(1)}, f32[16,64,512]{2,1,0:T(8,128)}, u32[]{:S(2)}) copy-start(f32[16,64,512]{2,1,0:T(8,128)} %get-tuple-element.26) | copy-start | bytes 6291460
  73.2 11.0 %copy-start.8 = (f32[1,16,64,512]{3,2,1,0:T(8,128)S(1)}, f32[1,16,64,512]{3,2,1,0:T(8,128)}, u32[]{:S(2)}) copy-start(f32[1,16,64,512]{3,2,1,0:T(8,128)} %get-tuple-element.27) | copy-start | bytes 6291460
  73.3 11.0 %copy-start.9 = (f32[1,16,64,512]{3,2,1,0:T(8,128)S(1)}, f32[1,16,64,512]{3,2,1,0:T(8,128)}, u32[]{:S(2)}) copy-start(f32[1,16,64,512]{3,2,1,0:T(8,128)} %get-tuple-element.28) | copy-start | bytes 6291460
  76.6 8.7 %collective-permute-start.13 = (f32[1,64,512]{2,1,0:T(8,128)S(1)}, f32[1,64,512]{2,1,0:T(8,128)S(1)}, u32[]{:S(2)}, u32[]{:S(2)}) collective-permute-start(f32[1,64,512]{2,1,0:T(8,128)S(1)} %get-tuple-element.19), channel_id=1, source_target_pairs={{4,0},{8,4},{12,8},{16,12},{20,16},{24,20},{28,24},{5,1},{9,5},{13... | collective-permute-start | bytes 393224 | tf_op jit(solution)/shard_map/ppermute | solution.py:20
  77.9 7.4 %collective-permute-start.12 = (f32[1,64,512]{2,1,0:T(8,128)S(1)}, f32[1,64,512]{2,1,0:T(8,128)S(1)}, u32[]{:S(2)}, u32[]{:S(2)}) collective-permute-start(f32[1,64,512]{2,1,0:T(8,128)S(1)} %get-tuple-element.18), channel_id=1, source_target_pairs={{0,4},{4,8},{8,12},{12,16},{16,20},{20,24},{24,28},{1,5},{5,9},{9,... | collective-permute-start | bytes 393224 | tf_op jit(solution)/shard_map/ppermute | solution.py:17
  85.4 19.9 %collective-permute-start.15 = (f32[18,1,512]{2,1,0:T(1,128)S(1)}, f32[18,1,512]{2,1,0:T(1,128)S(1)}, u32[]{:S(2)}, u32[]{:S(2)}) collective-permute-start(f32[18,1,512]{2,1,0:T(1,128)S(1)} %get-tuple-element.6), channel_id=1, source_target_pairs={{1,0},{2,1},{3,2},{5,4},{6,5},{7,6},{9,8},{10,9},{11,10},{13,12},{... | collective-permute-start | bytes 110600 | tf_op jit(solution)/shard_map/ppermute | solution.py:20
  87.3 18.0 %collective-permute-start.14 = (f32[18,1,512]{2,1,0:T(1,128)S(1)}, f32[18,1,512]{2,1,0:T(1,128)S(1)}, u32[]{:S(2)}, u32[]{:S(2)}) collective-permute-start(f32[18,1,512]{2,1,0:T(1,128)S(1)} %get-tuple-element.5), channel_id=1, source_target_pairs={{0,1},{1,2},{2,3},{4,5},{5,6},{6,7},{8,9},{9,10},{10,11},{12,13},{... | collective-permute-start | bytes 110600 | tf_op jit(solution)/shard_map/ppermute | solution.py:17
  95.3 25.3 %all-to-all-start = ((f32[8,1,16384]{2,1,0:T(1,128)}), f32[8,1,16384]{2,1,0:T(1,128)S(1)}, u32[]{:S(2)}, u32[]{:S(2)}) async-start(f32[8,1,16384]{2,1,0:T(1,128)} %reshape.111), calls=%async_computation | async-start | bytes 1048576 | tf_op jit(solution)/shard_map/all_to_all | solution.py:67
  120.6 19.6 %all-to-all-start.1 = ((f32[8,1,16384]{2,1,0:T(1,128)}), f32[8,1,16384]{2,1,0:T(1,128)S(1)}, u32[]{:S(2)}, u32[]{:S(2)}) async-start(f32[8,1,16384]{2,1,0:T(1,128)} %reshape.113), calls=%async_computation.1 | async-start | bytes 1048576 | tf_op jit(solution)/shard_map/all_to_all | solution.py:67
  (8 other events, 36.9 us)
where the time goes:
time: 145 us
  starting transfers between devices  59.6 us (41%)
  other arithmetic  47.4 us (33%)
  waiting for transfers between devices  22.9 us (16%)
  local copies, waits for them, and re-layouts  12.2 us (8%)
  between operations  1.99 us (1%)
    ppermute x8, starting transfers between devices, extended(): lax.ppermute(lax.slice_in_dim(block, block.shape[dim] - width, None, axis...  30.6 us
    sub x3, other arithmetic, update(): return center - step_size * rate  16.9 us
    ppermute x8, starting transfers between devices, extended(): lax.ppermute(lax.slice_in_dim(block, 0, width, axis=dim), axis, backward)  14.7 us
    all_to_all x2, starting transfers between devices, composite(): lax.all_to_all(packed, 'depth', split_axis=3, concat_axis=0, tiled=True)  14.3 us
    concatenate x4, other arithmetic, extended(): block = jnp.concatenate([low, block, high], axis=dim)  12.1 us
    all_to_all x2, waiting for transfers between devices, composite(): lax.all_to_all(packed, 'depth', split_axis=3, concat_axis=0, tiled=True)  11.3 us
    ppermute x8, waiting for transfers between devices, extended(): lax.ppermute(lax.slice_in_dim(block, block.shape[dim] - width, None, axis...  10.6 us
    unnamed x34, local copies, waits for them, and re-layouts  7.32 us
  transfers between devices with their start and end apart: 18, of which 8 were waited for; matrix products, arithmetic and copies ran while one was open for 18% of the time, Pallas kernels for 0%

commit v1 on v0

v1 whole, which is shorter than its diff:
```python
import functools

import jax
import jax.numpy as jnp
from jax import lax
from jax.experimental import pallas as pl
from jax.experimental.pallas import tpu as pltpu
from jax.sharding import PartitionSpec as P

STEPS = 4
step_size = 0.3
LANES = 128
SUB = 8
W = STEPS

VMEM = pl.BlockSpec(memory_space=pltpu.VMEM)
SMEM = pl.BlockSpec(memory_space=pltpu.SMEM)
FAR = pl.BlockSpec(memory_space=pltpu.HBM)


def f32(*shape):
    return jax.ShapeDtypeStruct(shape, jnp.float32)


def near(*shape):
    return pltpu.VMEM(shape, jnp.float32)


def resident(*arrays):
    return [pltpu.with_memory_space_constraint(a, pltpu.VMEM) for a in arrays]


def params(mib=None):
    if mib is None:
        return pltpu.CompilerParams()
    return pltpu.CompilerParams(vmem_limit_bytes=mib * 2**20)


def distant(*arrays):
    return [pltpu.with_memory_space_constraint(a, pltpu.HBM) for a in arrays]


def low_half(shape):
    return lax.broadcasted_iota(jnp.int32, shape, len(shape) - 2) < W


def is_even():
    return lax.rem(lax.axis_index("depth"), 2) == 0


def depth_pack_kernel(level, vel, cross, inner, sems):
    planes = level.shape[0]
    even = is_even()
    copies = []
    for n, (out, to_low) in enumerate(((cross, even), (inner, jnp.logical_not(even)))):
        z0 = jnp.where(to_low, 0, planes - W)
        v0 = jnp.where(to_low, 0, planes - W + 1)
        copies.append(pltpu.make_async_copy(level.at[pl.ds(z0, W)], out.at[pl.ds(0, W)], sems.at[n, 0]))
        for k in range(3):
            copies.append(
                pltpu.make_async_copy(
                    vel.at[k, pl.ds(v0, W - 1)],
                    out.at[pl.ds(W + (W - 1) * k, W - 1)],
                    sems.at[n, k + 1],
                )
            )
    for c in copies:
        c.start()
    for c in copies:
        c.wait()


def depth_pack(level, vel):
    planes, rows, cols = level.shape
    shape = near(W + 3 * (W - 1), rows, cols)
    return pl.pallas_call(
        depth_pack_kernel,
        out_shape=(shape, shape),
        in_specs=[FAR, FAR],
        out_specs=(VMEM, VMEM),
        scratch_shapes=[pltpu.SemaphoreType.DMA((2, 4))],
        compiler_params=params(6),
        name="depth_pack",
    )(*distant(level, vel))


def image_pack_kernel(level, vel, up1, down1, up2, down2, lev, ve, sems):
    planes, rows, _ = level.shape
    copies = []
    for s, r0 in enumerate((0, rows - SUB)):
        copies.append(pltpu.make_async_copy(level.at[:, pl.ds(r0, SUB), :], lev.at[s], sems.at[s, 0]))
        copies.append(pltpu.make_async_copy(vel.at[:, :, pl.ds(r0, SUB), :], ve.at[s], sems.at[s, 1]))
    for c in copies:
        c.start()
    for c in copies:
        c.wait()

    def emit(z, slot, up, down):
        low = low_half(lev.shape[-2:])
        half = lambda a: pltpu.roll(a, W, 0)
        down[slot, 0:SUB] = jnp.where(low, lev[0, z], half(ve[0, 0, z]))
        down[slot, SUB : 2 * SUB] = jnp.where(low, ve[0, 1, z], half(ve[0, 2, z]))
        up[slot, 0:SUB] = jnp.where(low, half(ve[1, 0, z]), lev[1, z])
        up[slot, SUB : 2 * SUB] = jnp.where(low, half(ve[1, 2, z]), ve[1, 1, z])

    def outer(j, c):
        emit(jnp.where(j < W, j, j + planes - 2 * W), j, up1, down1)
        return c

    def inner(j, c):
        emit(j + W, j, up2, down2)
        return c

    lax.fori_loop(0, 2 * W, outer, 0)
    lax.fori_loop(0, planes - 2 * W, inner, 0)


def image_pack(level, vel):
    planes, rows, cols = level.shape
    a = near(2 * W, 2 * SUB, cols)
    b = near(planes - 2 * W, 2 * SUB, cols)
    return pl.pallas_call(
        image_pack_kernel,
        out_shape=(a, a, b, b),
        in_specs=[FAR, FAR],
        out_specs=(VMEM,) * 4,
        scratch_shapes=[
            pltpu.VMEM((2, planes, SUB, cols), jnp.float32),
            pltpu.VMEM((2, 3, planes, SUB, cols), jnp.float32),
            pltpu.SemaphoreType.DMA((2, 2)),
        ],
        compiler_params=params(6),
        name="image_pack",
    )(*distant(level, vel))


def row_halos(hi, lo, slot):
    low = low_half((SUB, hi.shape[-1]))
    h0, h1, l0, l1 = hi[slot, 0:SUB], hi[slot, SUB : 2 * SUB], lo[slot, 0:SUB], lo[slot, SUB : 2 * SUB]
    return (
        jnp.where(low, h0, l0),
        pltpu.roll(jnp.where(low, l0, h0), W, 0),
        jnp.where(low, h1, l1),
        pltpu.roll(jnp.where(low, l1, h1), W, 0),
    )


def corner_pack_kernel(hi, lo, cross, inner):
    even = is_even()
    for out, to_low in ((cross, even), (inner, jnp.logical_not(even))):
        s0 = jnp.where(to_low, 0, W)
        first = jnp.where(to_low, 0, 1)
        for j in range(W):
            tiles = row_halos(hi, lo, s0 + j)
            out[j] = tiles[0]
            at = j - first

            @pl.when((at >= 0) & (at < W - 1))
            def _():
                for k in range(3):
                    out[W + (W - 1) * k + at] = tiles[k + 1]


def corner_pack(hi, lo):
    shape = near(W + 3 * (W - 1), SUB, hi.shape[-1])
    return pl.pallas_call(
        corner_pack_kernel,
        out_shape=(shape, shape),
        in_specs=[VMEM, VMEM],
        out_specs=(VMEM, VMEM),
        compiler_params=params(6),
        name="corner_pack",
    )(*resident(hi, lo))


def render(field, planes, rows, cols, flag, scale, out, sums):
    reverse = flag != 0
    sign = jnp.where(reverse, 1.0, -1.0).astype(jnp.float32)

    def tile(i, c):
        r0 = pl.multiple_of(i * SUB, SUB)
        total = jnp.zeros((SUB, cols), jnp.float32)
        last = jnp.ones((SUB, cols), jnp.float32)
        q = jnp.zeros((SUB, cols), jnp.float32)
        g = jnp.zeros((SUB, cols), jnp.float32)
        step = sign * scale
        for z in range(planes):
            f = field[z, pl.ds(r0, SUB), :]
            e = jnp.exp(-f * f)
            total = total + e * step
            now = jnp.exp(total)
            weight = now - last
            last = now
            q = q + weight * jnp.tanh(f)
            g = g + weight * e
        logs = -sign * total
        factor = jnp.where(reverse, jnp.exp(logs), -1.0)
        sums[0, pl.ds(r0, SUB), :] = q * factor
        sums[1, pl.ds(r0, SUB), :] = g * factor
        sums[2, pl.ds(r0, SUB), :] = logs
        return c

    lax.fori_loop(0, rows // SUB, tile, 0)


def spread(sums, out):
    _, rows, cols = sums.shape
    dests = out.shape[0]
    width = cols // dests
    groups = LANES // width
    part = rows // groups
    lane = lax.broadcasted_iota(jnp.int32, (part, LANES), 1)
    for d in range(dests):
        j, offset = divmod(d * width, LANES)
        for ch in range(3):
            value = None
            for n in range(groups):
                piece = sums[ch, n * part : (n + 1) * part, j * LANES : (j + 1) * LANES]
                shift = (n * width - offset) % LANES
                if shift:
                    piece = pltpu.roll(piece, shift, 1)
                value = piece if value is None else jnp.where(lane < n * width, value, piece)
            out[d, ch * part : (ch + 1) * part, :] = value


def first_kernel(flag, level, out, ext_f, sums, sem, *, scale):
    planes, rows, cols = level.shape
    a = pltpu.make_async_copy(level, ext_f.at[pl.ds(0, planes), pl.ds(0, rows), :], sem)
    a.start()
    a.wait()
    render(ext_f, planes, rows, cols, flag[lax.axis_index("depth")], scale, out, sums)
    spread(sums, out)


def first(level, flag, scale, dests):
    planes, rows, cols = level.shape
    ext = (planes + 2 * W, rows + SUB, cols)
    return pl.pallas_call(
        functools.partial(first_kernel, scale=scale),
        out_shape=(f32(dests, 3 * rows * cols // dests // LANES, LANES), near(*ext)),
        in_specs=[SMEM, FAR],
        out_specs=(VMEM, VMEM),
        scratch_shapes=[pltpu.VMEM((3, rows, cols), jnp.float32), pltpu.SemaphoreType.DMA],
        compiler_params=params(6),
        name="first",
    )(flag, *distant(level))


def side(tiles, j, lane, up):
    n = len(tiles)
    own = pltpu.roll(tiles[j], 1 if not up else LANES - 1, 1)
    k = j + 1 if up else j - 1
    if 0 <= k < n:
        other = pltpu.roll(tiles[k], 1 if not up else LANES - 1, 1)
    else:
        other = jnp.zeros_like(own)
    return jnp.where(lane == (LANES - 1 if up else 0), other, own)


def second_kernel(
    flag, ext_f, vel, cross, inner, ccross, cinner, hi1, lo1, hi2, lo2,
    out, level_out, f0, other, edge, sums, sem, *, scale,
):
    layers, all_rows, cols = ext_f.shape
    planes, rows = layers - 2 * W, all_rows - SUB
    even = is_even()

    for src, corner, low in ((cross, ccross, even), (inner, cinner, jnp.logical_not(even))):
        zf = jnp.where(low, planes + W, planes)
        for j in range(W):
            f0[zf + j, 0:rows] = src[j]
            f0[zf + j, rows : rows + SUB] = corner[j]

    def fill(z, slot, hi, lo):
        tiles = row_halos(hi, lo, slot)
        f0[z, rows : rows + SUB] = tiles[0]
        for k in range(3):
            edge[k, z] = tiles[k + 1]

    def fill_outer(j, c):
        fill(jnp.where(j < W, j, j + planes - 2 * W), j, hi1, lo1)
        return c

    def fill_inner(j, c):
        fill(j + W, j, hi2, lo2)
        return c

    lax.fori_loop(0, 2 * W, fill_outer, 0)
    lax.fori_loop(0, planes - 2 * W, fill_inner, 0)

    nt = all_rows // SUB
    nl = cols // LANES

    def layer(src, dst, z, row_tiles, speed):
        zi = jnp.where(z < 0, z + layers, z)
        zl = jnp.where(z < 1, z - 1 + layers, z - 1)
        zh = jnp.where(z < -1, z + 1 + layers, z + 1)
        sub = lax.broadcasted_iota(jnp.int32, (SUB, LANES), 0)
        lane = lax.broadcasted_iota(jnp.int32, (SUB, LANES), 1)
        first_sub = sub == 0
        last_sub = sub == SUB - 1
        for i in range(row_tiles):
            r = slice(i * SUB, (i + 1) * SUB)
            ru = slice((i + 1) % nt * SUB, ((i + 1) % nt + 1) * SUB)
            rd = slice((i - 1) % nt * SUB, ((i - 1) % nt + 1) * SUB)
            tiles = [src[zi, r, j * LANES : (j + 1) * LANES] for j in range(nl)]
            for j in range(nl):
                js = slice(j * LANES, (j + 1) * LANES)
                f = tiles[j]
                below = src[zi, rd, js]
                above = src[zi, ru, js]
                lows = (
                    lambda: src[zl, r, js],
                    lambda: jnp.where(first_sub, pltpu.roll(below, 1, 0), pltpu.roll(f, 1, 0)),
                    lambda: side(tiles, j, lane, False),
                )
                highs = (
                    lambda: src[zh, r, js],
                    lambda: jnp.where(last_sub, pltpu.roll(above, SUB - 1, 0), pltpu.roll(f, SUB - 1, 0)),
                    lambda: side(tiles, j, lane, True),
                )
                rate = None
                for k in range(3):
                    u = speed(k, i, js)
                    upwind = jnp.where(u > 0.0, lows[k](), highs[k]())
                    term = jnp.abs(u) * (upwind - f)
                    rate = term if rate is None else rate + term
                dst[zi, r, js] = f + step_size * rate

    def step(src, dst, t):
        reach = STEPS - t
        row_tiles = nt if reach else rows // SUB
        own_tiles = rows // SUB

        def own(z, c):
            def speed(k, i, js):
                if i == own_tiles:
                    return edge[k, z, :, js]
                return vel[k, z, i * SUB : (i + 1) * SUB, js]

            layer(src, dst, z, row_tiles, speed)
            return c

        lax.fori_loop(0, planes, own, 0)

        for halo, corner, low in ((cross, ccross, even), (inner, cinner, jnp.logical_not(even))):
            skip = jnp.where(low, W - 1 - reach, 0)
            base = jnp.where(low, -reach, planes)

            def outside(n, c):
                def speed(k, i, js):
                    at = W + (W - 1) * k + skip + n
                    if i == own_tiles:
                        return corner[at, :, js]
                    return halo[at, i * SUB : (i + 1) * SUB, js]

                layer(src, dst, base + n, row_tiles, speed)
                return c

            if reach:
                lax.fori_loop(0, reach, outside, 0)

    src, dst = f0, other
    for t in range(1, STEPS + 1):
        step(src, dst, t)
        src, dst = dst, src

    store = pltpu.make_async_copy(src.at[pl.ds(0, planes), pl.ds(0, rows), :], level_out, sem)
    store.start()
    render(src, planes, rows, cols, flag[lax.axis_index("depth")], scale, out, sums)
    spread(sums, out)
    store.wait()


def second(flag, ext_f, vel, halos, scale, dests):
    layers, all_rows, cols = ext_f.shape
    planes, rows = layers - 2 * W, all_rows - SUB
    return pl.pallas_call(
        functools.partial(second_kernel, scale=scale),
        out_shape=(
            f32(dests, 3 * rows * cols // dests // LANES, LANES),
            pltpu.HBM((planes, rows, cols), jnp.float32),
            near(*ext_f.shape),
        ),
        in_specs=[SMEM] + [VMEM] * 10,
        out_specs=(VMEM, FAR, VMEM),
        input_output_aliases={1: 2},
        scratch_shapes=[
            pltpu.VMEM(ext_f.shape, jnp.float32),
            pltpu.VMEM((3, planes, SUB, cols), jnp.float32),
            pltpu.VMEM((3, rows, cols), jnp.float32),
            pltpu.SemaphoreType.DMA,
        ],
        compiler_params=params(10),
        name="second",
    )(flag, *resident(ext_f, vel, *halos))[:2]


def composite_kernel(rank, parts, out):
    dests, stacked, _ = parts.shape
    part = stacked // 3
    _, rows, width = out.shape
    groups = rows // part
    for i in range(part // SUB):
        r = slice(i * SUB, (i + 1) * SUB)
        logs = [parts[e, 2 * part + i * SUB : 2 * part + (i + 1) * SUB, :] for e in range(dests)]
        q = g = total = None
        for b in range(dests):
            earlier = jnp.zeros((SUB, LANES), jnp.float32)
            for e in range(dests):
                if e != b:
                    earlier = earlier + jnp.where(rank[e] < rank[b], 1.0, 0.0) * logs[e]
            front = jnp.exp(earlier)
            qb = front * parts[b, r, :]
            gb = front * parts[b, part + i * SUB : part + (i + 1) * SUB, :]
            q = qb if q is None else q + qb
            g = gb if g is None else g + gb
            total = logs[b] if total is None else total + logs[b]
        alpha = 1.0 - jnp.exp(total)
        for ch, value in enumerate((0.5 * (alpha + q), g, 0.5 * (alpha - q), alpha)):
            for n in range(groups):
                piece = pltpu.roll(value, (LANES - n * width) % LANES, 1) if n else value
                out[ch, n * part + i * SUB : n * part + (i + 1) * SUB, :] = piece[:, :width]


def composite(rank, parts, rows, width):
    return pl.pallas_call(
        composite_kernel,
        out_shape=f32(4, rows, width),
        in_specs=[SMEM, VMEM],
        out_specs=VMEM,
        compiler_params=params(6),
        name="composite",
    )(rank, *resident(parts))


def local(level_set, velocity, view_flag, slab_rank):
    planes, rows, cols = level_set.shape
    depth = lax.axis_size("depth")
    image = lax.axis_size("image")
    scale = 2.0 / (planes * depth)
    width = cols // depth

    swap_inner = [(i, i ^ 1) for i in range(depth)]
    swap_cross = [p for i in range(1, depth - 1, 2) for p in ((i, i + 1), (i + 1, i))]
    up = [(i, i + 1) for i in range(image - 1)]
    down = [(b, a) for a, b in up]

    cross, inner = depth_pack(level_set, velocity)
    cross = lax.ppermute(cross, "depth", swap_cross)
    inner = lax.ppermute(inner, "depth", swap_inner)
    up1, down1, up2, down2 = image_pack(level_set, velocity)
    lo1 = lax.ppermute(up1, "image", up)
    hi1 = lax.ppermute(down1, "image", down)
    lo2 = lax.ppermute(up2, "image", up)
    hi2 = lax.ppermute(down2, "image", down)
    ccross, cinner = corner_pack(hi1, lo1)
    ccross = lax.ppermute(ccross, "depth", swap_cross)
    cinner = lax.ppermute(cinner, "depth", swap_inner)

    packed, ext_f = first(level_set, view_flag, scale, depth)
    parts = lax.all_to_all(packed, "depth", 0, 0, tiled=True)
    halos = (cross, inner, ccross, cinner, hi1, lo1, hi2, lo2)
    packed2, level_next = second(view_flag, ext_f, velocity, halos, scale, depth)
    parts2 = lax.all_to_all(packed2, "depth", 0, 0, tiled=True)
    image_first = composite(slab_rank, parts, rows, width)
    image_second = composite(slab_rank, parts2, rows, width)
    return (image_first, image_second, level_next)


def solution(mesh):
    placed = (P("depth", "image", None), P(None, "depth", "image", None), P(), P())
    return jax.shard_map(
        local,
        mesh=mesh,
        in_specs=placed,
        out_specs=(P(None, "image", "depth"), P(None, "image", "depth"), P("depth", "image", None)),
        check_vma=False,
    )
```

time: 145 us -> 83.2 us (0.57)
  other arithmetic: 47.4 us -> 0.01 us
  starting transfers between devices: 59.6 us -> 25.2 us
  Pallas kernels: 0 us -> 29.2 us
  local copies, waits for them, and re-layouts: 12.2 us -> 1.77 us
  waiting for transfers between devices: 22.9 us -> 25.8 us
    pallas_call x0 -> x7, Pallas kernels: none -> 29.2 us  [the longest x1 16.4 us: second(): pl.pallas_call(functools.partial(second_kernel, scale=scale), out_shape=(...]
    ppermute x16 -> x8, starting transfers between devices: 45.3 us -> 16.6 us  [the longest x1 4.23 us: local(): hi2 = lax.ppermute(down2, 'image', down)]
    sub x7 -> x0, other arithmetic: 16.9 us -> none  [the longest x3 16.9 us: update(): return center - step_size * rate]
    concatenate x6 -> x0, other arithmetic: 12.9 us -> none  [the longest x4 12.1 us: extended(): block = jnp.concatenate([low, block, high], axis=dim)]
    another operation x3 -> x0, other arithmetic: 8.03 us -> none  [the longest x1 5.46 us: render_brick(): jnp.stack([jax.nn.sigmoid(2.0 * field), jnp.exp(-field * field), jax.nn.s...]
    all_to_all x2, starting transfers between devices: 14.3 us -> 8.59 us  [the longest x1 4.72 us: local(): parts2 = lax.all_to_all(packed2, 'depth', 0, 0, tiled=True)]
    unnamed x34 -> x12, local copies, waits for them, and re-layouts: 7.32 us -> 1.77 us
    all_to_all x2 -> x0, other arithmetic: 3.77 us -> none  [composite(): lax.all_to_all(packed, 'depth', split_axis=3, concat_axis=0, tiled=True)]
  transfers between devices with their start and end apart: 18 -> 10, of which waited for: 8 -> 5; matrix products, arithmetic and copies ran while one was open for 18% -> 0% of each run, Pallas kernels for 0% -> 29%
where the time goes in v1:
time: 83.2 us; the launch traced here: 82.7 us
  Pallas kernels  29.2 us (35%)
  waiting for transfers between devices  25.8 us (31%)
  starting transfers between devices  25.2 us (30%)
  local copies, waits for them, and re-layouts  1.77 us (2%)
    pallas_call x1, Pallas kernels, second(): pl.pallas_call(functools.partial(second_kernel, scale=scale), out_shape=(...  16.4 us
    all_to_all x1, waiting for transfers between devices, local(): parts2 = lax.all_to_all(packed2, 'depth', 0, 0, tiled=True)  11.1 us
    ppermute x1, waiting for transfers between devices, local(): lo2 = lax.ppermute(up2, 'image', up)  6.13 us
    all_to_all x1, starting transfers between devices, local(): parts2 = lax.all_to_all(packed2, 'depth', 0, 0, tiled=True)  4.72 us
    pallas_call x1, Pallas kernels, first(): pl.pallas_call(functools.partial(first_kernel, scale=scale), out_shape=(f...  4.3 us
    ppermute x1, starting transfers between devices, local(): hi2 = lax.ppermute(down2, 'image', down)  4.23 us
    ppermute x1, waiting for transfers between devices, local(): hi2 = lax.ppermute(down2, 'image', down)  3.89 us
    all_to_all x1, starting transfers between devices, local(): parts = lax.all_to_all(packed, 'depth', 0, 0, tiled=True)  3.87 us
  transfers between devices with their start and end apart: 10, of which 5 were waited for; matrix products, arithmetic and copies ran while one was open for 0% of the time, Pallas kernels for 29%

profile of v1, /device:TPU:4, one launch (start us, length us, event | category | flops | bytes accessed | tf_op | source)
XLA Modules:
  0.0 82.7 jit_solution(6065810233511725947)
XLA Ops:
  0.6 3.8 %depth_pack.1 = (f32[13,64,512]{2,1,0:T(8,128)}, f32[13,64,512]{2,1,0:T(8,128)}) custom-call(f32[16,64,512]{2,1,0:T(8,128)} %level.5, f32[3,16,64,512]{3,2,1,0:T(8,128)} %vel.5), custom_call_target="tpu_custom_call" | custom-call | tf_op jit(solution)/shard_map/depth_pack/pallas_call | solution.py:76
  4.5 1.9 %collective-permute-start = (f32[13,64,512]{2,1,0:T(8,128)}, f32[13,64,512]{2,1,0:T(8,128)}, u32[]{:S(2)}, u32[]{:S(2)}) collective-permute-start(f32[13,64,512]{2,1,0:T(8,128)} %get-tuple-element.17), channel_id=1, source_target_pairs={{4,8},{8,4},{12,16},{16,12},{20,24},{24,20},{5,9},{9,5},{13,17},{1... | collective-permute-start | bytes 5111816 | tf_op jit(solution)/shard_map/ppermute | solution.py:450
  6.4 1.8 %collective-permute-start.1 = (f32[13,64,512]{2,1,0:T(8,128)}, f32[13,64,512]{2,1,0:T(8,128)}, u32[]{:S(2)}, u32[]{:S(2)}) collective-permute-start(f32[13,64,512]{2,1,0:T(8,128)} %get-tuple-element.18), channel_id=1, source_target_pairs={{0,4},{4,0},{8,12},{12,8},{16,20},{20,16},{24,28},{28,24},{1,5},{5... | collective-permute-start | bytes 5111816 | tf_op jit(solution)/shard_map/ppermute | solution.py:451
  8.2 4.3 %first.1 = (f32[8,96,128]{2,1,0:T(8,128)}, f32[24,72,512]{2,1,0:T(8,128)S(1)}) custom-call(s32[8]{0:T(128)S(1)} %copy-done.2, f32[16,64,512]{2,1,0:T(8,128)} %level.5), custom_call_target="tpu_custom_call" | custom-call | tf_op jit(solution)/shard_map/first/pallas_call | solution.py:238
  12.5 1.7 %copy-done = f32[24,72,512]{2,1,0:T(8,128)} copy-done((f32[24,72,512]{2,1,0:T(8,128)}, f32[24,72,512]{2,1,0:T(8,128)S(1)}, u32[]{:S(2)}) %copy-start) | copy-done | bytes 3538968
  14.2 3.9 %all-to-all-start = ((f32[8,96,128]{2,1,0:T(8,128)}), f32[8,96,128]{2,1,0:T(8,128)S(1)}, u32[]{:S(2)}, u32[]{:S(2)}) async-start(f32[8,96,128]{2,1,0:T(8,128)} %get-tuple-element.15), calls=%async_computation | async-start | bytes 786432 | tf_op jit(solution)/shard_map/all_to_all | solution.py:462
  18.1 1.9 %image_pack.1 = (f32[8,16,512]{2,1,0:T(8,128)S(1)}, f32[8,16,512]{2,1,0:T(8,128)S(1)}, f32[8,16,512]{2,1,0:T(8,128)S(1)}, f32[8,16,512]{2,1,0:T(8,128)S(1)}) custom-call(f32[16,64,512]{2,1,0:T(8,128)} %level.5, f32[3,16,64,512]{3,2,1,0:T(8,128)} %vel.5), custom_call_target="tpu_custom_call" | custom-call | tf_op jit(solution)/shard_map/image_pack/pallas_call | solution.py:122
  20.0 3.6 %collective-permute-start.2 = (f32[8,16,512]{2,1,0:T(8,128)S(1)}, f32[8,16,512]{2,1,0:T(8,128)S(1)}, u32[]{:S(2)}, u32[]{:S(2)}) collective-permute-start(f32[8,16,512]{2,1,0:T(8,128)S(1)} %get-tuple-element.19), channel_id=1, source_target_pairs={{1,0},{2,1},{3,2},{5,4},{6,5},{7,6},{9,8},{10,9},{11,10},{13,12},{... | collective-permute-start | bytes 786440 | tf_op jit(solution)/shard_map/ppermute | solution.py:454
  23.6 2.5 %collective-permute-start.3 = (f32[8,16,512]{2,1,0:T(8,128)S(1)}, f32[8,16,512]{2,1,0:T(8,128)S(1)}, u32[]{:S(2)}, u32[]{:S(2)}) collective-permute-start(f32[8,16,512]{2,1,0:T(8,128)S(1)} %get-tuple-element.20), channel_id=1, source_target_pairs={{0,1},{1,2},{2,3},{4,5},{5,6},{6,7},{8,9},{9,10},{10,11},{12,13},{... | collective-permute-start | bytes 786440 | tf_op jit(solution)/shard_map/ppermute | solution.py:453
  26.1 4.2 %collective-permute-start.6 = (f32[8,16,512]{2,1,0:T(8,128)S(1)}, f32[8,16,512]{2,1,0:T(8,128)S(1)}, u32[]{:S(2)}, u32[]{:S(2)}) collective-permute-start(f32[8,16,512]{2,1,0:T(8,128)S(1)} %get-tuple-element.23), channel_id=1, source_target_pairs={{1,0},{2,1},{3,2},{5,4},{6,5},{7,6},{9,8},{10,9},{11,10},{13,12},{... | collective-permute-start | bytes 786440 | tf_op jit(solution)/shard_map/ppermute | solution.py:456
  30.4 0.8 collective-permute-done.2.hi.hi1
  31.2 1.9 %collective-permute-start.7 = (f32[8,16,512]{2,1,0:T(8,128)S(1)}, f32[8,16,512]{2,1,0:T(8,128)S(1)}, u32[]{:S(2)}, u32[]{:S(2)}) collective-permute-start(f32[8,16,512]{2,1,0:T(8,128)S(1)} %get-tuple-element.24), channel_id=1, source_target_pairs={{0,1},{1,2},{2,3},{4,5},{5,6},{6,7},{8,9},{9,10},{10,11},{12,13},{... | collective-permute-start | bytes 786440 | tf_op jit(solution)/shard_map/ppermute | solution.py:455
  33.1 3.8 %collective-permute-done.3.lo.lo1 = f32[8,16,512]{2,1,0:T(8,128)S(1)} collective-permute-done((f32[8,16,512]{2,1,0:T(8,128)S(1)}, f32[8,16,512]{2,1,0:T(8,128)S(1)}, u32[]{:S(2)}, u32[]{:S(2)}) %collective-permute-start.3) | collective-permute-done | bytes 262176 | tf_op jit(solution)/shard_map/ppermute | solution.py:453
  36.9 0.7 collective-permute-start.4
  37.6 3.9 %collective-permute-done.6.hi2 = f32[8,16,512]{2,1,0:T(8,128)S(1)} collective-permute-done((f32[8,16,512]{2,1,0:T(8,128)S(1)}, f32[8,16,512]{2,1,0:T(8,128)S(1)}, u32[]{:S(2)}, u32[]{:S(2)}) %collective-permute-start.6) | collective-permute-done | bytes 262176 | tf_op jit(solution)/shard_map/ppermute | solution.py:456
  41.5 6.1 %collective-permute-done.7.lo2 = f32[8,16,512]{2,1,0:T(8,128)S(1)} collective-permute-done((f32[8,16,512]{2,1,0:T(8,128)S(1)}, f32[8,16,512]{2,1,0:T(8,128)S(1)}, u32[]{:S(2)}, u32[]{:S(2)}) %collective-permute-start.7) | collective-permute-done | bytes 262176 | tf_op jit(solution)/shard_map/ppermute | solution.py:455
  47.7 0.0 collective-permute-done.1.inner
  47.7 0.0 copy-start.3
  47.7 16.4 %second.1 = (f32[8,96,128]{2,1,0:T(8,128)}, f32[16,64,512]{2,1,0:T(8,128)}, f32[24,72,512]{2,1,0:T(8,128)S(1)}) custom-call(s32[8]{0:T(128)S(1)} %copy-done.2, f32[24,72,512]{2,1,0:T(8,128)S(1)} %copy-done.1, f32[3,16,64,512]{3,2,1,0:T(8,128)S(1)} %bitcast.1, f32[13,64,512]{2,1,0:T(8,128)} %collective-permute-done.cross, ...), custom_call_target="tpu_custom_call", output_to_operand_aliasing={{2}: (1, {})} | custom-call | tf_op jit(solution)/shard_map/second/pallas_call | solution.py:378
  64.1 0.0 all-to-all-done.parts
  64.1 4.7 %all-to-all-start.1 = ((f32[8,96,128]{2,1,0:T(8,128)}), f32[8,96,128]{2,1,0:T(8,128)S(1)}, u32[]{:S(2)}, u32[]{:S(2)}) async-start(f32[8,96,128]{2,1,0:T(8,128)} %get-tuple-element.25), calls=%async_computation.1 | async-start | bytes 786432 | tf_op jit(solution)/shard_map/all_to_all | solution.py:465
  68.8 1.4 %composite.2 = f32[4,64,64]{2,1,0:T(8,128)} custom-call(s32[8]{0:T(128)S(1)} %copy-done.3, f32[8,96,128]{2,1,0:T(8,128)S(1)} %all-to-all-done.parts), custom_call_target="tpu_custom_call" | custom-call | tf_op jit(solution)/shard_map/composite/pallas_call | solution.py:427
  70.2 11.1 %all-to-all-done.1.parts = f32[8,96,128]{2,1,0:T(8,128)S(1)} async-done(((f32[8,96,128]{2,1,0:T(8,128)}), f32[8,96,128]{2,1,0:T(8,128)S(1)}, u32[]{:S(2)}, u32[]{:S(2)}) %all-to-all-start.1) | async-done | bytes 393248 | tf_op jit(solution)/shard_map/all_to_all | solution.py:465
  81.3 1.4 %composite.3 = f32[4,64,64]{2,1,0:T(8,128)} custom-call(s32[8]{0:T(128)S(1)} %copy-done.3, f32[8,96,128]{2,1,0:T(8,128)S(1)} %all-to-all-done.1.parts), custom_call_target="tpu_custom_call" | custom-call | tf_op jit(solution)/shard_map/composite/pallas_call | solution.py:427
  (16 shorter events, 0.1 us)
Async XLA Ops:
  0.6 7.5 %copy-start.2 = (s32[8]{0:T(128)S(1)}, s32[8]{0:T(128)}, u32[]{:S(2)}) copy-start(s32[8]{0:T(128)} %flag.3) | copy-start | bytes 100
  4.5 43.2 %collective-permute-start = (f32[13,64,512]{2,1,0:T(8,128)}, f32[13,64,512]{2,1,0:T(8,128)}, u32[]{:S(2)}, u32[]{:S(2)}) collective-permute-start(f32[13,64,512]{2,1,0:T(8,128)} %get-tuple-element.17), channel_id=1, source_target_pairs={{4,8},{8,4},{12,16},{16,12},{20,24},{24,20},{5,9},{9,5},{13,17},{1... | collective-permute-start | bytes 5111816 | tf_op jit(solution)/shard_map/ppermute | solution.py:450
  6.4 41.3 %collective-permute-start.1 = (f32[13,64,512]{2,1,0:T(8,128)}, f32[13,64,512]{2,1,0:T(8,128)}, u32[]{:S(2)}, u32[]{:S(2)}) collective-permute-start(f32[13,64,512]{2,1,0:T(8,128)} %get-tuple-element.18), channel_id=1, source_target_pairs={{0,4},{4,0},{8,12},{12,8},{16,20},{20,16},{24,28},{28,24},{1,5},{5... | collective-permute-start | bytes 5111816 | tf_op jit(solution)/shard_map/ppermute | solution.py:451
  8.2 39.5 %slice-start = ((s8[6291456]{0:T(1024)(128)(4,1)}), s8[2097152]{0:T(1024)(128)(4,1)S(1)}, s32[]{:S(2)}) async-start(s8[6291456]{0:T(1024)(128)(4,1)} %bitcast), calls=%async_computation.2 | async-start | bytes 4194304
  12.5 1.8 %copy-start = (f32[24,72,512]{2,1,0:T(8,128)}, f32[24,72,512]{2,1,0:T(8,128)S(1)}, u32[]{:S(2)}) copy-start(f32[24,72,512]{2,1,0:T(8,128)S(1)} %get-tuple-element.16.ext_f) | copy-start | bytes 10616836
  14.2 49.9 %all-to-all-start = ((f32[8,96,128]{2,1,0:T(8,128)}), f32[8,96,128]{2,1,0:T(8,128)S(1)}, u32[]{:S(2)}, u32[]{:S(2)}) async-start(f32[8,96,128]{2,1,0:T(8,128)} %get-tuple-element.15), calls=%async_computation | async-start | bytes 786432 | tf_op jit(solution)/shard_map/all_to_all | solution.py:462
  18.1 29.6 %slice-start.1 = ((s8[6291456]{0:T(1024)(128)(4,1)}), s8[4194304]{0:T(1024)(128)(4,1)S(1)}, s32[]{:S(2)}) async-start(s8[6291456]{0:T(1024)(128)(4,1)} %bitcast), calls=%async_computation.3 | async-start | bytes 8388608
  18.1 29.6 %copy-start.1 = (f32[24,72,512]{2,1,0:T(8,128)S(1)}, f32[24,72,512]{2,1,0:T(8,128)}, u32[]{:S(2)}) copy-start(f32[24,72,512]{2,1,0:T(8,128)} %copy-done) | copy-start | bytes 10616836
  20.0 11.2 %collective-permute-start.2 = (f32[8,16,512]{2,1,0:T(8,128)S(1)}, f32[8,16,512]{2,1,0:T(8,128)S(1)}, u32[]{:S(2)}, u32[]{:S(2)}) collective-permute-start(f32[8,16,512]{2,1,0:T(8,128)S(1)} %get-tuple-element.19), channel_id=1, source_target_pairs={{1,0},{2,1},{3,2},{5,4},{6,5},{7,6},{9,8},{10,9},{11,10},{13,12},{... | collective-permute-start | bytes 786440 | tf_op jit(solution)/shard_map/ppermute | solution.py:454
  23.6 13.3 %collective-permute-start.3 = (f32[8,16,512]{2,1,0:T(8,128)S(1)}, f32[8,16,512]{2,1,0:T(8,128)S(1)}, u32[]{:S(2)}, u32[]{:S(2)}) collective-permute-start(f32[8,16,512]{2,1,0:T(8,128)S(1)} %get-tuple-element.20), channel_id=1, source_target_pairs={{0,1},{1,2},{2,3},{4,5},{5,6},{6,7},{8,9},{9,10},{10,11},{12,13},{... | collective-permute-start | bytes 786440 | tf_op jit(solution)/shard_map/ppermute | solution.py:453
  26.1 15.4 %collective-permute-start.6 = (f32[8,16,512]{2,1,0:T(8,128)S(1)}, f32[8,16,512]{2,1,0:T(8,128)S(1)}, u32[]{:S(2)}, u32[]{:S(2)}) collective-permute-start(f32[8,16,512]{2,1,0:T(8,128)S(1)} %get-tuple-element.23), channel_id=1, source_target_pairs={{1,0},{2,1},{3,2},{5,4},{6,5},{7,6},{9,8},{10,9},{11,10},{13,12},{... | collective-permute-start | bytes 786440 | tf_op jit(solution)/shard_map/ppermute | solution.py:456
  31.2 16.5 %collective-permute-start.7 = (f32[8,16,512]{2,1,0:T(8,128)S(1)}, f32[8,16,512]{2,1,0:T(8,128)S(1)}, u32[]{:S(2)}, u32[]{:S(2)}) collective-permute-start(f32[8,16,512]{2,1,0:T(8,128)S(1)} %get-tuple-element.24), channel_id=1, source_target_pairs={{0,1},{1,2},{2,3},{4,5},{5,6},{6,7},{8,9},{9,10},{10,11},{12,13},{... | collective-permute-start | bytes 786440 | tf_op jit(solution)/shard_map/ppermute | solution.py:455
  36.9 10.7 %collective-permute-start.4 = (f32[13,8,512]{2,1,0:T(8,128)S(1)}, f32[13,8,512]{2,1,0:T(8,128)S(1)}, u32[]{:S(2)}, u32[]{:S(2)}) collective-permute-start(f32[13,8,512]{2,1,0:T(8,128)S(1)} %get-tuple-element.21), channel_id=1, source_target_pairs={{4,8},{8,4},{12,16},{16,12},{20,24},{24,20},{5,9},{9,5},{13,17},{1... | collective-permute-start | bytes 638984 | tf_op jit(solution)/shard_map/ppermute | solution.py:458
  41.5 6.1 %collective-permute-start.5 = (f32[13,8,512]{2,1,0:T(8,128)S(1)}, f32[13,8,512]{2,1,0:T(8,128)S(1)}, u32[]{:S(2)}, u32[]{:S(2)}) collective-permute-start(f32[13,8,512]{2,1,0:T(8,128)S(1)} %get-tuple-element.22), channel_id=1, source_target_pairs={{0,4},{4,0},{8,12},{12,8},{16,20},{20,16},{24,28},{28,24},{1,5},{5... | collective-permute-start | bytes 638984 | tf_op jit(solution)/shard_map/ppermute | solution.py:459
  47.7 21.1 %copy-start.3 = (s32[8]{0:T(128)S(1)}, s32[8]{0:T(128)}, u32[]{:S(2)}) copy-start(s32[8]{0:T(128)} %rank.3) | copy-start | bytes 100
  64.1 17.2 %all-to-all-start.1 = ((f32[8,96,128]{2,1,0:T(8,128)}), f32[8,96,128]{2,1,0:T(8,128)S(1)}, u32[]{:S(2)}, u32[]{:S(2)}) async-start(f32[8,96,128]{2,1,0:T(8,128)} %get-tuple-element.25), calls=%async_computation.1 | async-start | bytes 786432 | tf_op jit(solution)/shard_map/all_to_all | solution.py:465

commit v2 on v1

v2 whole, which is shorter than its diff:
```python
import functools

import jax
import jax.numpy as jnp
from jax import lax
from jax.experimental import pallas as pl
from jax.experimental.pallas import tpu as pltpu
from jax.sharding import PartitionSpec as P


STEPS = 4
step_size = 0.3
LANES = 128
SUB = 8
W = STEPS

VMEM = pl.BlockSpec(memory_space=pltpu.VMEM)
SMEM = pl.BlockSpec(memory_space=pltpu.SMEM)
FAR = pl.BlockSpec(memory_space=pltpu.HBM)
LOOSE = pl.BlockSpec(memory_space=pl.ANY)


def f32(*shape):
    return jax.ShapeDtypeStruct(shape, jnp.float32)


def near(*shape):
    return pltpu.VMEM(shape, jnp.float32)


def resident(*arrays):
    return [pltpu.with_memory_space_constraint(a, pltpu.VMEM) for a in arrays]


def params(mib=None):
    if mib is None:
        return pltpu.CompilerParams()
    return pltpu.CompilerParams(vmem_limit_bytes=mib * 2**20)


def distant(*arrays):
    return [pltpu.with_memory_space_constraint(a, pltpu.HBM) for a in arrays]


def is_even():
    return lax.rem(lax.axis_index("depth"), 2) == 0


def depth_pack_kernel(level, vel, cross, inner, sems):
    planes = level.shape[0]
    even = is_even()
    copies = []
    for n, (out, to_low) in enumerate(((cross, even), (inner, jnp.logical_not(even)))):
        z0 = jnp.where(to_low, 0, planes - W)
        v0 = jnp.where(to_low, 0, planes - W + 1)
        copies.append(pltpu.make_async_copy(level.at[pl.ds(z0, W)], out.at[pl.ds(0, W)], sems.at[n, 0]))
        for k in range(3):
            copies.append(
                pltpu.make_async_copy(
                    vel.at[k, pl.ds(v0, W - 1)],
                    out.at[pl.ds(W + (W - 1) * k, W - 1)],
                    sems.at[n, k + 1],
                )
            )
    for c in copies:
        c.start()
    for c in copies:
        c.wait()


def depth_pack(level, vel):
    _, rows, cols = level.shape
    shape = near(W + 3 * (W - 1), rows, cols)
    return pl.pallas_call(
        depth_pack_kernel,
        out_shape=(shape, shape),
        in_specs=[FAR, FAR],
        out_specs=(VMEM, VMEM),
        scratch_shapes=[pltpu.SemaphoreType.DMA((2, 4))],
        compiler_params=params(6),
        name="depth_pack",
    )(*distant(level, vel))


HALO_ROWS = W + 3 * (W - 1)


def row_span(z, k=None):
    start = z * HALO_ROWS + (0 if k is None else W + (W - 1) * k)
    return slice(start, start + (W if k is None else W - 1))


def image_pack_kernel(level, vel, up, down, lev, ve, sems):
    planes, rows, _ = level.shape
    copies = []
    for s, r0 in enumerate((0, rows - SUB)):
        copies.append(pltpu.make_async_copy(level.at[:, pl.ds(r0, SUB), :], lev.at[s], sems.at[s, 0]))
        copies.append(pltpu.make_async_copy(vel.at[:, :, pl.ds(r0, SUB), :], ve.at[s], sems.at[s, 1]))
    for c in copies:
        c.start()
    for c in copies:
        c.wait()

    for z in range(planes):
        down[row_span(z)] = lev[0, z, 0:W]
        up[row_span(z)] = lev[1, z, SUB - W : SUB]
        for k in range(3):
            down[row_span(z, k)] = ve[0, k, z, 0 : W - 1]
            up[row_span(z, k)] = ve[1, k, z, SUB - W + 1 : SUB]


def image_pack(level, vel):
    planes, _, cols = level.shape
    shape = near(planes * HALO_ROWS, cols)
    return pl.pallas_call(
        image_pack_kernel,
        out_shape=(shape, shape),
        in_specs=[FAR, FAR],
        out_specs=(VMEM, VMEM),
        scratch_shapes=[
            pltpu.VMEM((2, planes, SUB, cols), jnp.float32),
            pltpu.VMEM((2, 3, planes, SUB, cols), jnp.float32),
            pltpu.SemaphoreType.DMA((2, 2)),
        ],
        compiler_params=params(6),
        name="image_pack",
    )(*distant(level, vel))


def put_row_halos(field, speeds, hi, lo, z):
    field[0:W] = hi[row_span(z)]
    field[W:SUB] = lo[row_span(z)]
    for k, speed in enumerate(speeds):
        speed[...] = jnp.zeros(speed.shape, jnp.float32)
        speed[0 : W - 1] = hi[row_span(z, k)]
        speed[SUB - W + 1 : SUB] = lo[row_span(z, k)]


def corner_pack_kernel(hi, lo, cross, inner):
    planes = hi.shape[0] // HALO_ROWS
    even = is_even()

    def pack(low, high):
        for out, first, skip in ((low, 0, 0), (high, planes - W, 1)):
            for j in range(W):
                at = j - skip
                speeds = []
                if 0 <= at < W - 1:
                    speeds = [out.at[W + (W - 1) * k + at] for k in range(3)]
                put_row_halos(out.at[j], speeds, hi, lo, first + j)

    @pl.when(even)
    def _():
        pack(cross, inner)

    @pl.when(jnp.logical_not(even))
    def _():
        pack(inner, cross)


def corner_pack(hi, lo):
    shape = near(W + 3 * (W - 1), SUB, hi.shape[-1])
    return pl.pallas_call(
        corner_pack_kernel,
        out_shape=(shape, shape),
        in_specs=[VMEM, VMEM],
        out_specs=(VMEM, VMEM),
        compiler_params=params(6),
        name="corner_pack",
    )(*resident(hi, lo))


def render(field, planes, rows, cols, flag, scale, sums):
    reverse = flag != 0
    sign = jnp.where(reverse, 1.0, -1.0).astype(jnp.float32)

    def tile(i, c):
        r0 = pl.multiple_of(i * SUB, SUB)
        total = jnp.zeros((SUB, cols), jnp.float32)
        last = jnp.ones((SUB, cols), jnp.float32)
        q = jnp.zeros((SUB, cols), jnp.float32)
        g = jnp.zeros((SUB, cols), jnp.float32)
        step = sign * scale
        for z in range(planes):
            f = field[z, pl.ds(r0, SUB), :]
            e = jnp.exp(-f * f)
            total = total + e * step
            now = jnp.exp(total)
            weight = now - last
            last = now
            q = q + weight * jnp.tanh(f)
            g = g + weight * e
        logs = -sign * total
        factor = jnp.where(reverse, jnp.exp(logs), -1.0)
        sums[0, pl.ds(r0, SUB), :] = q * factor
        sums[1, pl.ds(r0, SUB), :] = g * factor
        sums[2, pl.ds(r0, SUB), :] = logs
        return c

    lax.fori_loop(0, rows // SUB, tile, 0)


def spread(sums, out, stage, sem):
    _, rows, cols = sums.shape
    dests = out.shape[0]
    copies = []
    width = cols // dests
    groups = LANES // width
    part = rows // groups
    lane = lax.broadcasted_iota(jnp.int32, (part, LANES), 1)
    for d in range(dests):
        j, offset = divmod(d * width, LANES)
        for ch in range(3):
            value = None
            for n in range(groups):
                piece = sums[ch, n * part : (n + 1) * part, j * LANES : (j + 1) * LANES]
                shift = (n * width - offset) % LANES
                if shift:
                    piece = pltpu.roll(piece, shift, 1)
                value = piece if value is None else jnp.where(lane < n * width, value, piece)
            stage[d, ch * part : (ch + 1) * part, :] = value
        copies.append(pltpu.make_async_copy(stage.at[d], out.at[d], sem.at[d]))
        copies[-1].start()
    return copies


def first_kernel(flag, level, after, out, sums, stage, sent, *, scale):
    planes, rows, cols = level.shape
    render(level, planes, rows, cols, flag[lax.axis_index("depth")], scale, sums)
    for c in spread(sums, out, stage, sent):
        c.wait()


def first(level, flag, after, scale, dests):
    _, rows, cols = level.shape
    packed = (dests, 3 * rows * cols // dests // LANES, LANES)
    return pl.pallas_call(
        functools.partial(first_kernel, scale=scale),
        out_shape=pltpu.HBM(packed, jnp.float32),
        in_specs=[SMEM, VMEM, LOOSE],
        out_specs=FAR,
        scratch_shapes=[
            pltpu.VMEM((3, rows, cols), jnp.float32),
            pltpu.VMEM(packed, jnp.float32),
            pltpu.SemaphoreType.DMA((dests,)),
        ],
        compiler_params=params(6),
        name="first",
    )(flag, *resident(level), after)


def side(tiles, j, lane, up):
    n = len(tiles)
    own = pltpu.roll(tiles[j], 1 if not up else LANES - 1, 1)
    k = j + 1 if up else j - 1
    if 0 <= k < n:
        other = pltpu.roll(tiles[k], 1 if not up else LANES - 1, 1)
    else:
        other = jnp.zeros_like(own)
    return jnp.where(lane == (LANES - 1 if up else 0), other, own)


def layer(src, dst, z, row_tiles, speed):
    layers, all_rows, cols = src.shape
    nt = all_rows // SUB
    nl = cols // LANES
    zi = jnp.where(z < 0, z + layers, z)
    zl = jnp.where(z < 1, z - 1 + layers, z - 1)
    zh = jnp.where(z < -1, z + 1 + layers, z + 1)
    sub = lax.broadcasted_iota(jnp.int32, (SUB, LANES), 0)
    lane = lax.broadcasted_iota(jnp.int32, (SUB, LANES), 1)
    first_sub = sub == 0
    last_sub = sub == SUB - 1
    for i in range(row_tiles):
        r = slice(i * SUB, (i + 1) * SUB)
        ru = slice((i + 1) % nt * SUB, ((i + 1) % nt + 1) * SUB)
        rd = slice((i - 1) % nt * SUB, ((i - 1) % nt + 1) * SUB)
        tiles = [src[zi, r, j * LANES : (j + 1) * LANES] for j in range(nl)]
        for j in range(nl):
            js = slice(j * LANES, (j + 1) * LANES)
            f = tiles[j]
            below = src[zi, rd, js]
            above = src[zi, ru, js]
            lows = (
                lambda: src[zl, r, js],
                lambda: jnp.where(first_sub, pltpu.roll(below, 1, 0), pltpu.roll(f, 1, 0)),
                lambda: side(tiles, j, lane, False),
            )
            highs = (
                lambda: src[zh, r, js],
                lambda: jnp.where(last_sub, pltpu.roll(above, SUB - 1, 0), pltpu.roll(f, SUB - 1, 0)),
                lambda: side(tiles, j, lane, True),
            )
            rate = None
            for k in range(3):
                u = speed(k, i, js)
                upwind = jnp.where(u > 0.0, lows[k](), highs[k]())
                term = jnp.abs(u) * (upwind - f)
                rate = term if rate is None else rate + term
            dst[zi, r, js] = f + step_size * rate


def own_layer(src, dst, z, row_tiles, vel, edge):
    own_tiles = vel.shape[2] // SUB

    def speed(k, i, js):
        if i == own_tiles:
            return edge[k, z, :, js]
        return vel[k, z, i * SUB : (i + 1) * SUB, js]

    layer(src, dst, z, row_tiles, speed)


def early_kernel(
    level, speeds, cross, inner, hi, lo, after,
    f0, f1, vel, hcross, hinner, edge, sems, arrived,
):
    layers, all_rows, _ = f0.shape
    planes, rows = layers - 2 * W, all_rows - SUB
    even = is_even()

    streams = [
        pltpu.make_async_copy(speeds.at[:, z], vel.at[:, z], arrived.at[z]) for z in range(planes)
    ]
    copies = [streams[0], streams[-1]]
    for n, (src, halo, low) in enumerate(((cross, hcross, even), (inner, hinner, jnp.logical_not(even)))):
        zf = jnp.where(low, planes + W, planes)
        copies.append(
            pltpu.make_async_copy(
                src.at[pl.ds(0, W)], f0.at[pl.ds(zf, W), pl.ds(0, rows), :], sems.at[n, 0]
            )
        )
        copies.append(pltpu.make_async_copy(src.at[pl.ds(W, 3 * (W - 1))], halo, sems.at[n, 1]))
    for c in streams[1:-1] + copies:
        c.start()

    def fill(z, c):
        f0[z, 0:rows] = level[z]
        return c

    lax.fori_loop(0, planes, fill, 0)
    for z in range(planes):
        put_row_halos(f0.at[z, rows : rows + SUB], [edge.at[k, z] for k in range(3)], hi, lo, z)

    def arriving(z, c):
        pltpu.make_async_copy(speeds.at[:, z], vel.at[:, z], arrived.at[z]).wait()
        own_layer(f0, f1, z, all_rows // SUB, vel, edge)
        return c

    lax.fori_loop(1, planes - 1, arriving, 0)
    for c in copies:
        c.wait()


def early(level, vel, cross, inner, hi, lo, after):
    planes, rows, cols = level.shape
    ext = (planes + 2 * W, rows + SUB, cols)
    halo = (3 * (W - 1), rows, cols)
    return pl.pallas_call(
        early_kernel,
        out_shape=(
            near(*ext), near(*ext), near(*vel.shape), near(*halo), near(*halo), near(3, planes, SUB, cols)
        ),
        in_specs=[VMEM, FAR, LOOSE, LOOSE, VMEM, VMEM, LOOSE],
        out_specs=(VMEM,) * 6,
        scratch_shapes=[pltpu.SemaphoreType.DMA((2, 2)), pltpu.SemaphoreType.DMA((planes,))],
        compiler_params=params(20),
        name="early",
    )(*resident(level), *distant(vel), cross, inner, *resident(hi, lo), after)


def second_kernel(
    flag, f0, f1, vel, hcross, hinner, edge, ccross, cinner,
    out, level_out, f0_out, f1_out, sums, stage, sem, sent, *, scale,
):
    layers, all_rows, cols = f0.shape
    planes, rows = layers - 2 * W, all_rows - SUB
    nt = all_rows // SUB
    own_tiles = rows // SUB
    even = is_even()
    sides = ((hcross, ccross, even), (hinner, cinner, jnp.logical_not(even)))

    for _, corner, low in sides:
        zf = jnp.where(low, planes + W, planes)
        for j in range(W):
            f0_out[zf + j, rows : rows + SUB] = corner[j]

    def step(src, dst, t):
        reach = STEPS - t
        row_tiles = nt if reach else own_tiles

        def own(z, c):
            own_layer(src, dst, z, row_tiles, vel, edge)
            return c

        if t == 1:
            lax.fori_loop(0, 2, lambda n, c: own(n * (planes - 1), c), 0)
        else:
            lax.fori_loop(0, planes, own, 0)

        for halo, corner, low in sides:
            skip = jnp.where(low, W - 1 - reach, 0)
            base = jnp.where(low, -reach, planes)

            def outside(n, c):
                def speed(k, i, js):
                    at = (W - 1) * k + skip + n
                    if i == own_tiles:
                        return corner[W + at, :, js]
                    return halo[at, i * SUB : (i + 1) * SUB, js]

                layer(src, dst, base + n, row_tiles, speed)
                return c

            if reach:
                lax.fori_loop(0, reach, outside, 0)

    src, dst = f0_out, f1_out
    for t in range(1, STEPS + 1):
        step(src, dst, t)
        src, dst = dst, src

    store = pltpu.make_async_copy(src.at[pl.ds(0, planes), pl.ds(0, rows), :], level_out, sem)
    store.start()
    render(src, planes, rows, cols, flag[lax.axis_index("depth")], scale, sums)
    for c in spread(sums, out, stage, sent):
        c.wait()
    store.wait()


def second(flag, state, corners, scale, dests):
    ext = state[0].shape
    _, planes, rows, cols = state[2].shape
    packed = (dests, 3 * rows * cols // dests // LANES, LANES)
    return pl.pallas_call(
        functools.partial(second_kernel, scale=scale),
        out_shape=(
            pltpu.HBM(packed, jnp.float32),
            pltpu.HBM((planes, rows, cols), jnp.float32),
            near(*ext),
            near(*ext),
        ),
        in_specs=[SMEM] + [VMEM] * 8,
        out_specs=(FAR, FAR, VMEM, VMEM),
        input_output_aliases={1: 2, 2: 3},
        scratch_shapes=[
            pltpu.VMEM((3, rows, cols), jnp.float32),
            pltpu.VMEM(packed, jnp.float32),
            pltpu.SemaphoreType.DMA,
            pltpu.SemaphoreType.DMA((dests,)),
        ],
        compiler_params=params(20),
        name="second",
    )(flag, *resident(*state, *corners))[:2]


def composite_kernel(rank, parts, out):
    dests, stacked, _ = parts.shape
    part = stacked // 3
    _, rows, width = out.shape
    groups = rows // part
    for i in range(part // SUB):
        r = slice(i * SUB, (i + 1) * SUB)
        logs = [parts[e, 2 * part + i * SUB : 2 * part + (i + 1) * SUB, :] for e in range(dests)]
        q = g = total = None
        for b in range(dests):
            earlier = jnp.zeros((SUB, LANES), jnp.float32)
            for e in range(dests):
                if e != b:
                    earlier = earlier + jnp.where(rank[e] < rank[b], 1.0, 0.0) * logs[e]
            front = jnp.exp(earlier)
            qb = front * parts[b, r, :]
            gb = front * parts[b, part + i * SUB : part + (i + 1) * SUB, :]
            q = qb if q is None else q + qb
            g = gb if g is None else g + gb
            total = logs[b] if total is None else total + logs[b]
        alpha = 1.0 - jnp.exp(total)
        for ch, value in enumerate((0.5 * (alpha + q), g, 0.5 * (alpha - q), alpha)):
            for n in range(groups):
                piece = pltpu.roll(value, (LANES - n * width) % LANES, 1) if n else value
                out[ch, n * part + i * SUB : n * part + (i + 1) * SUB, :] = piece[:, :width]


def composite(rank, parts, rows, width):
    return pl.pallas_call(
        composite_kernel,
        out_shape=f32(4, rows, width),
        in_specs=[SMEM, VMEM],
        out_specs=VMEM,
        compiler_params=params(6),
        name="composite",
    )(rank, *resident(parts))


def program(level_set, velocity, view_flag, slab_rank):
    planes, rows, cols = level_set.shape
    depth = lax.axis_size("depth")
    image = lax.axis_size("image")
    scale = 2.0 / (planes * depth)
    width = cols // depth

    swap_inner = [(i, i ^ 1) for i in range(depth)]
    swap_cross = [p for i in range(1, depth - 1, 2) for p in ((i, i + 1), (i + 1, i))]
    up = [(i, i + 1) for i in range(image - 1)]
    down = [(b, a) for a, b in up]

    cross, inner = depth_pack(level_set, velocity)
    cross = lax.ppermute(cross, "depth", swap_cross)
    inner = lax.ppermute(inner, "depth", swap_inner)
    to_up, to_down = image_pack(level_set, velocity)
    lo = lax.ppermute(to_up, "image", up)
    hi = lax.ppermute(to_down, "image", down)
    ccross, cinner = corner_pack(hi, lo)
    state = early(level_set, velocity, cross, inner, hi, lo, ccross)
    ccross = lax.ppermute(ccross, "depth", swap_cross)
    cinner = lax.ppermute(cinner, "depth", swap_inner)

    packed = first(level_set, view_flag, to_up, scale, depth)
    parts = lax.all_to_all(packed, "depth", 0, 0, tiled=True)
    packed2, level_next = second(view_flag, state, (ccross, cinner), scale, depth)
    parts2 = lax.all_to_all(packed2, "depth", 0, 0, tiled=True)
    image_first = composite(slab_rank, parts, rows, width)
    image_second = composite(slab_rank, parts2, rows, width)
    return (image_first, image_second, level_next)


def solution(mesh):
    placed = (P("depth", "image", None), P(None, "depth", "image", None), P(), P())
    return jax.shard_map(
        program,
        mesh=mesh,
        in_specs=placed,
        out_specs=(P(None, "image", "depth"), P(None, "image", "depth"), P("depth", "image", None)),
        check_vma=False,
    )
```

time: 83.2 us -> 78 us (0.938)
  starting transfers between devices: 25.2 us -> 21.3 us
  waiting for transfers between devices: 25.8 us -> 28.5 us
  Pallas kernels: 29.2 us -> 27 us
  local copies, waits for them, and re-layouts: 1.77 us -> 0.01 us
    ppermute x8 -> x6, starting transfers between devices: 16.6 us -> 10.3 us  [the longest x1 3.33 us: program(): hi = lax.ppermute(to_down, 'image', down)]
    pallas_call x1, Pallas kernels: 16.4 us -> 12 us  [second(): pl.pallas_call(functools.partial(second_kernel, scale=scale), out_shape=(...]
    ppermute x8 -> x6, waiting for transfers between devices: 14.6 us -> 17.3 us  [the longest x1 9.07 us: program(): lo = lax.ppermute(to_up, 'image', up)]
    all_to_all x2, starting transfers between devices: 8.59 us -> 11 us  [the longest x1 7.15 us: program(): parts2 = lax.all_to_all(packed2, 'depth', 0, 0, tiled=True)]
    pallas_call x2 -> x3, Pallas kernels: 6.19 us -> 8.39 us  [the longest x1 3.99 us: early(): pl.pallas_call(early_kernel, out_shape=(near(*ext), near(*ext), near(*vel...]
    unnamed x12 -> x6, local copies, waits for them, and re-layouts: 1.77 us -> 0.01 us
  transfers between devices with their start and end apart: 10 -> 8, of which waited for: 5 -> 3; matrix products, arithmetic and copies ran while one was open for 0% -> 0% of each run, Pallas kernels for 29% -> 28%
where the time goes in v2:
time: 78 us; the launch traced here: 77.6 us
  waiting for transfers between devices  28.5 us (37%)
  Pallas kernels  27 us (35%)
  starting transfers between devices  21.3 us (27%)
  between operations  0.78 us (1%)
    pallas_call x1, Pallas kernels, second(): pl.pallas_call(functools.partial(second_kernel, scale=scale), out_shape=(...  12 us
    all_to_all x1, waiting for transfers between devices, program(): parts2 = lax.all_to_all(packed2, 'depth', 0, 0, tiled=True)  11.1 us
    ppermute x1, waiting for transfers between devices, program(): lo = lax.ppermute(to_up, 'image', up)  9.07 us
    ppermute x1, waiting for transfers between devices, program(): hi = lax.ppermute(to_down, 'image', down)  8.24 us
    all_to_all x1, starting transfers between devices, program(): parts2 = lax.all_to_all(packed2, 'depth', 0, 0, tiled=True)  7.15 us
    pallas_call x1, Pallas kernels, early(): pl.pallas_call(early_kernel, out_shape=(near(*ext), near(*ext), near(*vel...  3.99 us
    all_to_all x1, starting transfers between devices, program(): parts = lax.all_to_all(packed, 'depth', 0, 0, tiled=True)  3.88 us
    pallas_call x1, Pallas kernels, depth_pack(): pl.pallas_call(depth_pack_kernel, out_shape=(shape, shape), in_specs=[FAR...  3.76 us
  transfers between devices with their start and end apart: 8, of which 3 were waited for; matrix products, arithmetic and copies ran while one was open for 0% of the time, Pallas kernels for 28%

profile of v2, /device:TPU:4, one launch (start us, length us, event | category | flops | bytes accessed | tf_op | source)
XLA Modules:
  0.0 77.6 jit_solution(13406385831208936470)
XLA Ops:
  0.6 3.8 %depth_pack.1 = (f32[13,64,512]{2,1,0:T(8,128)}, f32[13,64,512]{2,1,0:T(8,128)}) custom-call(f32[16,64,512]{2,1,0:T(8,128)} %level.7, f32[3,16,64,512]{3,2,1,0:T(8,128)} %speeds.1), custom_call_target="tpu_custom_call" | custom-call | tf_op jit(solution)/shard_map/depth_pack/pallas_call | solution.py:74
  4.4 1.8 %collective-permute-start = (f32[13,64,512]{2,1,0:T(8,128)}, f32[13,64,512]{2,1,0:T(8,128)}, u32[]{:S(2)}, u32[]{:S(2)}) collective-permute-start(f32[13,64,512]{2,1,0:T(8,128)} %get-tuple-element.18), channel_id=1, source_target_pairs={{4,8},{8,4},{12,16},{16,12},{20,24},{24,20},{5,9},{9,5},{13,17},{1... | collective-permute-start | bytes 5111816 | tf_op jit(solution)/shard_map/ppermute | solution.py:508
  6.2 1.8 %collective-permute-start.1 = (f32[13,64,512]{2,1,0:T(8,128)}, f32[13,64,512]{2,1,0:T(8,128)}, u32[]{:S(2)}, u32[]{:S(2)}) collective-permute-start(f32[13,64,512]{2,1,0:T(8,128)} %get-tuple-element.19), channel_id=1, source_target_pairs={{0,4},{4,0},{8,12},{12,8},{16,20},{20,16},{24,28},{28,24},{1,5},{5... | collective-permute-start | bytes 5111816 | tf_op jit(solution)/shard_map/ppermute | solution.py:509
  8.1 1.8 %image_pack.1 = (f32[208,512]{1,0:T(8,128)S(1)}, f32[208,512]{1,0:T(8,128)S(1)}) custom-call(f32[16,64,512]{2,1,0:T(8,128)} %level.7, f32[3,16,64,512]{3,2,1,0:T(8,128)} %speeds.1), custom_call_target="tpu_custom_call" | custom-call | tf_op jit(solution)/shard_map/image_pack/pallas_call | solution.py:115
  9.9 2.6 %first.1 = f32[8,96,128]{2,1,0:T(8,128)} custom-call(s32[8]{0:T(128)S(1)} %copy-done.1, f32[16,64,512]{2,1,0:T(8,128)S(1)} %copy-done, f32[208,512]{1,0:T(8,128)S(1)} %get-tuple-element.17.after), custom_call_target="tpu_custom_call" | custom-call | tf_op jit(solution)/shard_map/first/pallas_call | solution.py:237
  12.5 3.9 %all-to-all-start = ((f32[8,96,128]{2,1,0:T(8,128)}), f32[8,96,128]{2,1,0:T(8,128)S(1)}, u32[]{:S(2)}, u32[]{:S(2)}) async-start(f32[8,96,128]{2,1,0:T(8,128)} %first.1), calls=%async_computation | async-start | bytes 786432 | tf_op jit(solution)/shard_map/all_to_all | solution.py:519
  16.4 3.3 %collective-permute-start.2 = (f32[208,512]{1,0:T(8,128)S(1)}, f32[208,512]{1,0:T(8,128)S(1)}, u32[]{:S(2)}, u32[]{:S(2)}) collective-permute-start(f32[208,512]{1,0:T(8,128)S(1)} %get-tuple-element.20), channel_id=1, source_target_pairs={{1,0},{2,1},{3,2},{5,4},{6,5},{7,6},{9,8},{10,9},{11,10},{13,12},{... | collective-permute-start | bytes 1277960 | tf_op jit(solution)/shard_map/ppermute | solution.py:512
  19.7 2.5 %collective-permute-start.3 = (f32[208,512]{1,0:T(8,128)S(1)}, f32[208,512]{1,0:T(8,128)S(1)}, u32[]{:S(2)}, u32[]{:S(2)}) collective-permute-start(f32[208,512]{1,0:T(8,128)S(1)} %get-tuple-element.17.after), channel_id=1, source_target_pairs={{0,1},{1,2},{2,3},{4,5},{5,6},{6,7},{8,9},{9,10},{10,11},{12,13},{... | collective-permute-start | bytes 1277960 | tf_op jit(solution)/shard_map/ppermute | solution.py:511
  22.3 8.2 %collective-permute-done.2.hi = f32[208,512]{1,0:T(8,128)S(1)} collective-permute-done((f32[208,512]{1,0:T(8,128)S(1)}, f32[208,512]{1,0:T(8,128)S(1)}, u32[]{:S(2)}, u32[]{:S(2)}) %collective-permute-start.2) | collective-permute-done | bytes 426016 | tf_op jit(solution)/shard_map/ppermute | solution.py:512
  30.5 9.1 %collective-permute-done.3.lo = f32[208,512]{1,0:T(8,128)S(1)} collective-permute-done((f32[208,512]{1,0:T(8,128)S(1)}, f32[208,512]{1,0:T(8,128)S(1)}, u32[]{:S(2)}, u32[]{:S(2)}) %collective-permute-start.3) | collective-permute-done | bytes 426016 | tf_op jit(solution)/shard_map/ppermute | solution.py:511
  39.6 0.1 corner_pack.1
  39.7 0.1 collective-permute-start.5
  39.8 0.7 collective-permute-start.4
  40.5 0.0 collective-permute-done.cross
  40.5 0.0 collective-permute-done.1.inner
  40.5 4.0 %early.1 = (f32[24,72,512]{2,1,0:T(8,128)S(1)}, f32[24,72,512]{2,1,0:T(8,128)S(1)}, f32[3,16,64,512]{3,2,1,0:T(8,128)S(1)}, f32[9,64,512]{2,1,0:T(8,128)S(1)}, f...) custom-call(f32[16,64,512]{2,1,0:T(8,128)S(1)} %copy-done, f32[3,16,64,512]{3,2,1,0:T(8,128)} %speeds.1, ...), custom_call_target="tpu_custom_call" | custom-call | tf_op jit(solution)/shard_map/early/pallas_call | solution.py:359
  44.5 0.0 collective-permute-done.5.cinner
  44.5 0.0 collective-permute-done.4.ccross
  44.5 0.0 copy-start.2
  44.5 12.0 %second.1 = (f32[8,96,128]{2,1,0:T(8,128)}, f32[16,64,512]{2,1,0:T(8,128)}, f32[24,72,512]{2,1,0:T(8,128)S(1)}, f32[24,72,512]{2,1,0:T(8,128)S(1)}) custom-call(s32[8]{0:T(128)S(1)} %copy-done.1, f32[24,72,512]{2,1,0:T(8,128)S(1)} %get-tuple-element.22.f0, f32[24,72,512]{2,1,0:T(8,128)S(1)} %get-tuple-element.23.f1, ...), custom_call_target="tpu_custom_call", output_to_operand_aliasing={{2}: (1, {}), {3}: (2, {})} | custom-call | tf_op jit(solution)/shard_map/second/pallas_call | solution.py:435
  56.5 7.2 %all-to-all-start.1 = ((f32[8,96,128]{2,1,0:T(8,128)}), f32[8,96,128]{2,1,0:T(8,128)S(1)}, u32[]{:S(2)}, u32[]{:S(2)}) async-start(f32[8,96,128]{2,1,0:T(8,128)} %get-tuple-element.29), calls=%async_computation.1 | async-start | bytes 786432 | tf_op jit(solution)/shard_map/all_to_all | solution.py:521
  63.7 1.4 %composite.2 = f32[4,64,64]{2,1,0:T(8,128)} custom-call(s32[8]{0:T(128)S(1)} %copy-done.2, f32[8,96,128]{2,1,0:T(8,128)S(1)} %all-to-all-done.parts), custom_call_target="tpu_custom_call" | custom-call | tf_op jit(solution)/shard_map/composite/pallas_call | solution.py:485
  65.1 11.1 %all-to-all-done.1.parts = f32[8,96,128]{2,1,0:T(8,128)S(1)} async-done(((f32[8,96,128]{2,1,0:T(8,128)}), f32[8,96,128]{2,1,0:T(8,128)S(1)}, u32[]{:S(2)}, u32[]{:S(2)}) %all-to-all-start.1) | async-done | bytes 393248 | tf_op jit(solution)/shard_map/all_to_all | solution.py:521
  76.2 1.4 %composite.3 = f32[4,64,64]{2,1,0:T(8,128)} custom-call(s32[8]{0:T(128)S(1)} %copy-done.2, f32[8,96,128]{2,1,0:T(8,128)S(1)} %all-to-all-done.1.parts), custom_call_target="tpu_custom_call" | custom-call | tf_op jit(solution)/shard_map/composite/pallas_call | solution.py:485
  (6 shorter events, 0.0 us)
Async XLA Ops:
  4.4 36.1 %collective-permute-start = (f32[13,64,512]{2,1,0:T(8,128)}, f32[13,64,512]{2,1,0:T(8,128)}, u32[]{:S(2)}, u32[]{:S(2)}) collective-permute-start(f32[13,64,512]{2,1,0:T(8,128)} %get-tuple-element.18), channel_id=1, source_target_pairs={{4,8},{8,4},{12,16},{16,12},{20,24},{24,20},{5,9},{9,5},{13,17},{1... | collective-permute-start | bytes 5111816 | tf_op jit(solution)/shard_map/ppermute | solution.py:508
  6.2 3.7 %copy-start = (f32[16,64,512]{2,1,0:T(8,128)S(1)}, f32[16,64,512]{2,1,0:T(8,128)}, u32[]{:S(2)}) copy-start(f32[16,64,512]{2,1,0:T(8,128)} %level.7) | copy-start | bytes 6291460
  6.2 3.7 %copy-start.1 = (s32[8]{0:T(128)S(1)}, s32[8]{0:T(128)}, u32[]{:S(2)}) copy-start(s32[8]{0:T(128)} %flag.3) | copy-start | bytes 100
  6.2 34.2 %collective-permute-start.1 = (f32[13,64,512]{2,1,0:T(8,128)}, f32[13,64,512]{2,1,0:T(8,128)}, u32[]{:S(2)}, u32[]{:S(2)}) collective-permute-start(f32[13,64,512]{2,1,0:T(8,128)} %get-tuple-element.19), channel_id=1, source_target_pairs={{0,4},{4,0},{8,12},{12,8},{16,20},{20,16},{24,28},{28,24},{1,5},{5... | collective-permute-start | bytes 5111816 | tf_op jit(solution)/shard_map/ppermute | solution.py:509
  12.5 44.0 %all-to-all-start = ((f32[8,96,128]{2,1,0:T(8,128)}), f32[8,96,128]{2,1,0:T(8,128)S(1)}, u32[]{:S(2)}, u32[]{:S(2)}) async-start(f32[8,96,128]{2,1,0:T(8,128)} %first.1), calls=%async_computation | async-start | bytes 786432 | tf_op jit(solution)/shard_map/all_to_all | solution.py:519
  16.4 14.1 %collective-permute-start.2 = (f32[208,512]{1,0:T(8,128)S(1)}, f32[208,512]{1,0:T(8,128)S(1)}, u32[]{:S(2)}, u32[]{:S(2)}) collective-permute-start(f32[208,512]{1,0:T(8,128)S(1)} %get-tuple-element.20), channel_id=1, source_target_pairs={{1,0},{2,1},{3,2},{5,4},{6,5},{7,6},{9,8},{10,9},{11,10},{13,12},{... | collective-permute-start | bytes 1277960 | tf_op jit(solution)/shard_map/ppermute | solution.py:512
  19.7 19.8 %collective-permute-start.3 = (f32[208,512]{1,0:T(8,128)S(1)}, f32[208,512]{1,0:T(8,128)S(1)}, u32[]{:S(2)}, u32[]{:S(2)}) collective-permute-start(f32[208,512]{1,0:T(8,128)S(1)} %get-tuple-element.17.after), channel_id=1, source_target_pairs={{0,1},{1,2},{2,3},{4,5},{5,6},{6,7},{8,9},{9,10},{10,11},{12,13},{... | collective-permute-start | bytes 1277960 | tf_op jit(solution)/shard_map/ppermute | solution.py:511
  39.7 4.8 %collective-permute-start.5 = (f32[13,8,512]{2,1,0:T(8,128)S(1)}, f32[13,8,512]{2,1,0:T(8,128)S(1)}, u32[]{:S(2)}, u32[]{:S(2)}) collective-permute-start(f32[13,8,512]{2,1,0:T(8,128)S(1)} %get-tuple-element.28), channel_id=1, source_target_pairs={{0,4},{4,0},{8,12},{12,8},{16,20},{20,16},{24,28},{28,24},{1,5},{5... | collective-permute-start | bytes 638984 | tf_op jit(solution)/shard_map/ppermute | solution.py:516
  39.8 4.7 %collective-permute-start.4 = (f32[13,8,512]{2,1,0:T(8,128)S(1)}, f32[13,8,512]{2,1,0:T(8,128)S(1)}, u32[]{:S(2)}, u32[]{:S(2)}) collective-permute-start(f32[13,8,512]{2,1,0:T(8,128)S(1)} %get-tuple-element.21.after), channel_id=1, source_target_pairs={{4,8},{8,4},{12,16},{16,12},{20,24},{24,20},{5,9},{9,5},{13,17},{1... | collective-permute-start | bytes 638984 | tf_op jit(solution)/shard_map/ppermute | solution.py:515
  44.5 19.2 %copy-start.2 = (s32[8]{0:T(128)S(1)}, s32[8]{0:T(128)}, u32[]{:S(2)}) copy-start(s32[8]{0:T(128)} %rank.3) | copy-start | bytes 100
  56.5 19.7 %all-to-all-start.1 = ((f32[8,96,128]{2,1,0:T(8,128)}), f32[8,96,128]{2,1,0:T(8,128)S(1)}, u32[]{:S(2)}, u32[]{:S(2)}) async-start(f32[8,96,128]{2,1,0:T(8,128)} %get-tuple-element.29), calls=%async_computation.1 | async-start | bytes 786432 | tf_op jit(solution)/shard_map/all_to_all | solution.py:521

commit v3 on v2

--- a/solution.py
+++ b/solution.py
@@ -12,6 +12,7 @@
 step_size = 0.3
 LANES = 128
 SUB = 8
+EARLY = 3
 W = STEPS
 
 VMEM = pl.BlockSpec(memory_space=pltpu.VMEM)
@@ -260,7 +261,7 @@
     return jnp.where(lane == (LANES - 1 if up else 0), other, own)
 
 
-def layer(src, dst, z, row_tiles, speed):
+def layer(src, dst, z, tiles_done, speed):
     layers, all_rows, cols = src.shape
     nt = all_rows // SUB
     nl = cols // LANES
@@ -271,7 +272,7 @@
     lane = lax.broadcasted_iota(jnp.int32, (SUB, LANES), 1)
     first_sub = sub == 0
     last_sub = sub == SUB - 1
-    for i in range(row_tiles):
+    for i in tiles_done:
         r = slice(i * SUB, (i + 1) * SUB)
         ru = slice((i + 1) % nt * SUB, ((i + 1) % nt + 1) * SUB)
         rd = slice((i - 1) % nt * SUB, ((i - 1) % nt + 1) * SUB)
@@ -311,18 +312,52 @@
     layer(src, dst, z, row_tiles, speed)
 
 
+def stage_kernel(level, speeds, f0, f1, vel, arrived):
+    planes, rows, _ = level.shape
+    streams = [
+        pltpu.make_async_copy(speeds.at[:, z], vel.at[:, z], arrived.at[z]) for z in range(planes)
+    ]
+    for c in streams[1:-1] + [streams[0], streams[-1]]:
+        c.start()
+
+    def fill(z, c):
+        f0[z, 0:rows] = level[z]
+        return c
+
+    lax.fori_loop(0, planes, fill, 0)
+
+    def arriving(z, c):
+        pltpu.make_async_copy(speeds.at[:, z], vel.at[:, z], arrived.at[z]).wait()
+        own_layer(f0, f1, z, range(1, rows // SUB - 1), vel, None)
+        return c
+
+    lax.fori_loop(1, planes - 1, arriving, 0)
+    streams[0].wait()
+    streams[-1].wait()
+
+
+def stage(level, vel):
+    planes, rows, cols = level.shape
+    ext = (planes + 2 * W, rows + SUB, cols)
+    return pl.pallas_call(
+        stage_kernel,
+        out_shape=(near(*ext), near(*ext), near(*vel.shape)),
+        in_specs=[VMEM, FAR],
+        out_specs=(VMEM,) * 3,
+        scratch_shapes=[pltpu.SemaphoreType.DMA((planes,))],
+        compiler_params=params(16),
+        name="stage",
+    )(*resident(level), *distant(vel))
+
+
 def early_kernel(
-    level, speeds, cross, inner, hi, lo, after,
-    f0, f1, vel, hcross, hinner, edge, sems, arrived,
+    f0_in, f1_in, vel, cross, inner, hi, lo, after, f0, f1, hcross, hinner, edge, sems
 ):
     layers, all_rows, _ = f0.shape
     planes, rows = layers - 2 * W, all_rows - SUB
+    own_tiles = rows // SUB
     even = is_even()
-
-    streams = [
-        pltpu.make_async_copy(speeds.at[:, z], vel.at[:, z], arrived.at[z]) for z in range(planes)
-    ]
-    copies = [streams[0], streams[-1]]
+    copies = []
     for n, (src, halo, low) in enumerate(((cross, hcross, even), (inner, hinner, jnp.logical_not(even)))):
         zf = jnp.where(low, planes + W, planes)
         copies.append(
@@ -331,42 +366,40 @@
             )
         )
         copies.append(pltpu.make_async_copy(src.at[pl.ds(W, 3 * (W - 1))], halo, sems.at[n, 1]))
-    for c in streams[1:-1] + copies:
+    for c in copies:
         c.start()
-
-    def fill(z, c):
-        f0[z, 0:rows] = level[z]
-        return c
-
-    lax.fori_loop(0, planes, fill, 0)
     for z in range(planes):
         put_row_halos(f0.at[z, rows : rows + SUB], [edge.at[k, z] for k in range(3)], hi, lo, z)
 
-    def arriving(z, c):
-        pltpu.make_async_copy(speeds.at[:, z], vel.at[:, z], arrived.at[z]).wait()
-        own_layer(f0, f1, z, all_rows // SUB, vel, edge)
-        return c
-
-    lax.fori_loop(1, planes - 1, arriving, 0)
+    src, dst = f0, f1
+    for t in range(1, EARLY + 1):
+        done = (0, own_tiles - 1, own_tiles) if t == 1 else range(own_tiles + 1)
+
+        def own(z, c):
+            own_layer(src, dst, z, done, vel, edge)
+            return c
+
+        lax.fori_loop(t, planes - t, own, 0)
+        src, dst = dst, src
     for c in copies:
         c.wait()
 
 
-def early(level, vel, cross, inner, hi, lo, after):
-    planes, rows, cols = level.shape
-    ext = (planes + 2 * W, rows + SUB, cols)
+def early(staged, cross, inner, hi, lo, after):
+    ext = staged[0].shape
+    _, planes, rows, cols = staged[2].shape
     halo = (3 * (W - 1), rows, cols)
-    return pl.pallas_call(
+    out = pl.pallas_call(
         early_kernel,
-        out_shape=(
-            near(*ext), near(*ext), near(*vel.shape), near(*halo), near(*halo), near(3, planes, SUB, cols)
-        ),
-        in_specs=[VMEM, FAR, LOOSE, LOOSE, VMEM, VMEM, LOOSE],
-        out_specs=(VMEM,) * 6,
-        scratch_shapes=[pltpu.SemaphoreType.DMA((2, 2)), pltpu.SemaphoreType.DMA((planes,))],
+        out_shape=(near(*ext), near(*ext), near(*halo), near(*halo), near(3, planes, SUB, cols)),
+        in_specs=[VMEM, VMEM, VMEM, LOOSE, LOOSE, VMEM, VMEM, LOOSE],
+        out_specs=(VMEM,) * 5,
+        input_output_aliases={0: 0, 1: 1},
+        scratch_shapes=[pltpu.SemaphoreType.DMA((2, 2))],
         compiler_params=params(20),
         name="early",
-    )(*resident(level), *distant(vel), cross, inner, *resident(hi, lo), after)
+    )(*resident(*staged), cross, inner, *resident(hi, lo), after)
+    return (out[0], out[1], staged[2], *out[2:])
 
 
 def second_kernel(
@@ -387,14 +420,14 @@
 
     def step(src, dst, t):
         reach = STEPS - t
-        row_tiles = nt if reach else own_tiles
+        row_tiles = range(nt if reach else own_tiles)
 
         def own(z, c):
             own_layer(src, dst, z, row_tiles, vel, edge)
             return c
 
-        if t == 1:
-            lax.fori_loop(0, 2, lambda n, c: own(n * (planes - 1), c), 0)
+        if t <= EARLY:
+            lax.fori_loop(0, 2 * t, lambda n, c: own(jnp.where(n < t, n, n + planes - 2 * t), c), 0)
         else:
             lax.fori_loop(0, planes, own, 0)
 
@@ -511,7 +544,8 @@
     lo = lax.ppermute(to_up, "image", up)
     hi = lax.ppermute(to_down, "image", down)
     ccross, cinner = corner_pack(hi, lo)
-    state = early(level_set, velocity, cross, inner, hi, lo, ccross)
+    staged = stage(level_set, velocity)
+    state = early(staged, cross, inner, hi, lo, ccross)
     ccross = lax.ppermute(ccross, "depth", swap_cross)
     cinner = lax.ppermute(cinner, "depth", swap_inner)
 

time: 78 us -> 78.5 us (level)
  Pallas kernels: 27 us -> 28 us
    pallas_call x1 -> x2, Pallas kernels: 3.99 us -> 8.25 us  [the longest x1 5.28 us: early(): pl.pallas_call(early_kernel, out_shape=(near(*ext), near(*ext), near(*hal...]
    all_to_all x1, starting transfers between devices: 7.15 us -> 3.65 us  [program(): parts2 = lax.all_to_all(packed2, 'depth', 0, 0, tiled=True)]
    pallas_call x1, Pallas kernels: 12 us -> 8.71 us  [second(): pl.pallas_call(functools.partial(second_kernel, scale=scale), out_shape=(...]
    ppermute x1, starting transfers between devices: 0.07 us -> 3.05 us  [program(): cinner = lax.ppermute(cinner, 'depth', swap_inner)]
  transfers between devices with their start and end apart: 8 -> 8, of which waited for: 3 -> 3; matrix products, arithmetic and copies ran while one was open for 0% -> 0% of each run, Pallas kernels for 28% -> 29%
where the time goes in v3:
time: 78.5 us; the launch traced here: 78.1 us
  waiting for transfers between devices  28.5 us (36%)
  Pallas kernels  28 us (36%)
  starting transfers between devices  20.8 us (26%)
    all_to_all x1, waiting for transfers between devices, program(): parts2 = lax.all_to_all(packed2, 'depth', 0, 0, tiled=True)  11.1 us
    ppermute x1, waiting for transfers between devices, program(): lo = lax.ppermute(to_up, 'image', up)  9.07 us
    pallas_call x1, Pallas kernels, second(): pl.pallas_call(functools.partial(second_kernel, scale=scale), out_shape=(...  8.71 us
    ppermute x1, waiting for transfers between devices, program(): hi = lax.ppermute(to_down, 'image', down)  8.24 us
    pallas_call x1, Pallas kernels, early(): pl.pallas_call(early_kernel, out_shape=(near(*ext), near(*ext), near(*hal...  5.28 us
    all_to_all x1, starting transfers between devices, program(): parts = lax.all_to_all(packed, 'depth', 0, 0, tiled=True)  3.88 us
    pallas_call x1, Pallas kernels, depth_pack(): pl.pallas_call(depth_pack_kernel, out_shape=(shape, shape), in_specs=[FAR...  3.77 us
    all_to_all x1, starting transfers between devices, program(): parts2 = lax.all_to_all(packed2, 'depth', 0, 0, tiled=True)  3.65 us
  transfers between devices with their start and end apart: 8, of which 3 were waited for; matrix products, arithmetic and copies ran while one was open for 0% of the time, Pallas kernels for 29%

profile of v3, /device:TPU:4, one launch (start us, length us, event | category | flops | bytes accessed | tf_op | source)
XLA Modules:
  0.0 78.1 jit_solution(872425096200950365)
XLA Ops:
  0.6 3.8 %depth_pack.1 = (f32[13,64,512]{2,1,0:T(8,128)}, f32[13,64,512]{2,1,0:T(8,128)}) custom-call(f32[16,64,512]{2,1,0:T(8,128)} %level.7, f32[3,16,64,512]{3,2,1,0:T(8,128)} %vel.3), custom_call_target="tpu_custom_call" | custom-call | tf_op jit(solution)/shard_map/depth_pack/pallas_call | solution.py:75
  4.4 1.9 %collective-permute-start = (f32[13,64,512]{2,1,0:T(8,128)}, f32[13,64,512]{2,1,0:T(8,128)}, u32[]{:S(2)}, u32[]{:S(2)}) collective-permute-start(f32[13,64,512]{2,1,0:T(8,128)} %get-tuple-element.23), channel_id=1, source_target_pairs={{4,8},{8,4},{12,16},{16,12},{20,24},{24,20},{5,9},{9,5},{13,17},{1... | collective-permute-start | bytes 5111816 | tf_op jit(solution)/shard_map/ppermute | solution.py:541
  6.3 1.8 %collective-permute-start.1 = (f32[13,64,512]{2,1,0:T(8,128)}, f32[13,64,512]{2,1,0:T(8,128)}, u32[]{:S(2)}, u32[]{:S(2)}) collective-permute-start(f32[13,64,512]{2,1,0:T(8,128)} %get-tuple-element.24), channel_id=1, source_target_pairs={{0,4},{4,0},{8,12},{12,8},{16,20},{20,16},{24,28},{28,24},{1,5},{5... | collective-permute-start | bytes 5111816 | tf_op jit(solution)/shard_map/ppermute | solution.py:542
  8.1 1.8 %image_pack.1 = (f32[208,512]{1,0:T(8,128)S(1)}, f32[208,512]{1,0:T(8,128)S(1)}) custom-call(f32[16,64,512]{2,1,0:T(8,128)} %level.7, f32[3,16,64,512]{3,2,1,0:T(8,128)} %vel.3), custom_call_target="tpu_custom_call" | custom-call | tf_op jit(solution)/shard_map/image_pack/pallas_call | solution.py:116
  9.9 2.6 %first.1 = f32[8,96,128]{2,1,0:T(8,128)} custom-call(s32[8]{0:T(128)S(1)} %copy-done.1, f32[16,64,512]{2,1,0:T(8,128)S(1)} %copy-done, f32[208,512]{1,0:T(8,128)S(1)} %get-tuple-element.19.after), custom_call_target="tpu_custom_call" | custom-call | tf_op jit(solution)/shard_map/first/pallas_call | solution.py:238
  12.6 3.9 %all-to-all-start = ((f32[8,96,128]{2,1,0:T(8,128)}), f32[8,96,128]{2,1,0:T(8,128)S(1)}, u32[]{:S(2)}, u32[]{:S(2)}) async-start(f32[8,96,128]{2,1,0:T(8,128)} %first.1), calls=%async_computation | async-start | bytes 786432 | tf_op jit(solution)/shard_map/all_to_all | solution.py:553
  16.4 3.3 %collective-permute-start.2 = (f32[208,512]{1,0:T(8,128)S(1)}, f32[208,512]{1,0:T(8,128)S(1)}, u32[]{:S(2)}, u32[]{:S(2)}) collective-permute-start(f32[208,512]{1,0:T(8,128)S(1)} %get-tuple-element.25), channel_id=1, source_target_pairs={{1,0},{2,1},{3,2},{5,4},{6,5},{7,6},{9,8},{10,9},{11,10},{13,12},{... | collective-permute-start | bytes 1277960 | tf_op jit(solution)/shard_map/ppermute | solution.py:545
  19.8 2.5 %collective-permute-start.3 = (f32[208,512]{1,0:T(8,128)S(1)}, f32[208,512]{1,0:T(8,128)S(1)}, u32[]{:S(2)}, u32[]{:S(2)}) collective-permute-start(f32[208,512]{1,0:T(8,128)S(1)} %get-tuple-element.19.after), channel_id=1, source_target_pairs={{0,1},{1,2},{2,3},{4,5},{5,6},{6,7},{8,9},{9,10},{10,11},{12,13},{... | collective-permute-start | bytes 1277960 | tf_op jit(solution)/shard_map/ppermute | solution.py:544
  22.3 8.2 %collective-permute-done.2.hi = f32[208,512]{1,0:T(8,128)S(1)} collective-permute-done((f32[208,512]{1,0:T(8,128)S(1)}, f32[208,512]{1,0:T(8,128)S(1)}, u32[]{:S(2)}, u32[]{:S(2)}) %collective-permute-start.2) | collective-permute-done | bytes 426016 | tf_op jit(solution)/shard_map/ppermute | solution.py:545
  30.5 9.1 %collective-permute-done.3.lo = f32[208,512]{1,0:T(8,128)S(1)} collective-permute-done((f32[208,512]{1,0:T(8,128)S(1)}, f32[208,512]{1,0:T(8,128)S(1)}, u32[]{:S(2)}, u32[]{:S(2)}) %collective-permute-start.3) | collective-permute-done | bytes 426016 | tf_op jit(solution)/shard_map/ppermute | solution.py:544
  39.6 0.1 corner_pack.1
  39.7 0.7 collective-permute-start.4
  40.4 3.0 %collective-permute-start.5 = (f32[13,8,512]{2,1,0:T(8,128)S(1)}, f32[13,8,512]{2,1,0:T(8,128)S(1)}, u32[]{:S(2)}, u32[]{:S(2)}) collective-permute-start(f32[13,8,512]{2,1,0:T(8,128)S(1)} %get-tuple-element.32), channel_id=1, source_target_pairs={{0,4},{4,0},{8,12},{12,8},{16,20},{20,16},{24,28},{28,24},{1,5},{5... | collective-permute-start | bytes 638984 | tf_op jit(solution)/shard_map/ppermute | solution.py:550
  43.5 3.0 %stage.1 = (f32[24,72,512]{2,1,0:T(8,128)S(1)}, f32[24,72,512]{2,1,0:T(8,128)S(1)}, f32[3,16,64,512]{3,2,1,0:T(8,128)S(1)}) custom-call(f32[16,64,512]{2,1,0:T(8,128)S(1)} %copy-done, f32[3,16,64,512]{3,2,1,0:T(8,128)} %vel.3), custom_call_target="tpu_custom_call" | custom-call | tf_op jit(solution)/shard_map/stage/pallas_call | solution.py:342
  46.4 0.0 collective-permute-done.cross
  46.5 5.3 %early.1 = (f32[24,72,512]{2,1,0:T(8,128)S(1)}, f32[24,72,512]{2,1,0:T(8,128)S(1)}, f32[9,64,512]{2,1,0:T(8,128)S(1)}, f32[9,64,512]{2,1,0:T(8,128)S(1)}, f32[3,16,8,512]{3,2,1,0:T(8,128)S(1)}) custom-call(f32[24,72,512]{2,1,0:T(8,128)S(1)} %get-tuple-element.20.f0_in, ...), custom_call_target="tpu_custom_call", output_to_operand_aliasing={{0}: (0, {}), {1}: (1, {})} | custom-call | tf_op jit(solution)/shard_map/early/pallas_call | solution.py:392
  51.8 0.0 collective-permute-done.5.cinner
  51.8 0.0 copy-start.2
  51.8 8.7 %second.1 = (f32[8,96,128]{2,1,0:T(8,128)}, f32[16,64,512]{2,1,0:T(8,128)}, f32[24,72,512]{2,1,0:T(8,128)S(1)}, f32[24,72,512]{2,1,0:T(8,128)S(1)}) custom-call(s32[8]{0:T(128)S(1)} %copy-done.1, f32[24,72,512]{2,1,0:T(8,128)S(1)} %get-tuple-element.27.f0, f32[24,72,512]{2,1,0:T(8,128)S(1)} %get-tuple-element.28.f1, ...), custom_call_target="tpu_custom_call", output_to_operand_aliasing={{2}: (1, {}), {3}: (2, {})} | custom-call | tf_op jit(solution)/shard_map/second/pallas_call | solution.py:468
  60.5 0.0 all-to-all-done.parts
  60.5 3.7 %all-to-all-start.1 = ((f32[8,96,128]{2,1,0:T(8,128)}), f32[8,96,128]{2,1,0:T(8,128)S(1)}, u32[]{:S(2)}, u32[]{:S(2)}) async-start(f32[8,96,128]{2,1,0:T(8,128)} %get-tuple-element.33), calls=%async_computation.1 | async-start | bytes 786432 | tf_op jit(solution)/shard_map/all_to_all | solution.py:555
  64.2 1.4 %composite.2 = f32[4,64,64]{2,1,0:T(8,128)} custom-call(s32[8]{0:T(128)S(1)} %copy-done.2, f32[8,96,128]{2,1,0:T(8,128)S(1)} %all-to-all-done.parts), custom_call_target="tpu_custom_call" | custom-call | tf_op jit(solution)/shard_map/composite/pallas_call | solution.py:518
  65.6 11.1 %all-to-all-done.1.parts = f32[8,96,128]{2,1,0:T(8,128)S(1)} async-done(((f32[8,96,128]{2,1,0:T(8,128)}), f32[8,96,128]{2,1,0:T(8,128)S(1)}, u32[]{:S(2)}, u32[]{:S(2)}) %all-to-all-start.1) | async-done | bytes 393248 | tf_op jit(solution)/shard_map/all_to_all | solution.py:555
  76.7 1.4 %composite.3 = f32[4,64,64]{2,1,0:T(8,128)} custom-call(s32[8]{0:T(128)S(1)} %copy-done.2, f32[8,96,128]{2,1,0:T(8,128)S(1)} %all-to-all-done.1.parts), custom_call_target="tpu_custom_call" | custom-call | tf_op jit(solution)/shard_map/composite/pallas_call | solution.py:518
  (7 shorter events, 0.0 us)
Async XLA Ops:
  4.4 42.0 %collective-permute-start = (f32[13,64,512]{2,1,0:T(8,128)}, f32[13,64,512]{2,1,0:T(8,128)}, u32[]{:S(2)}, u32[]{:S(2)}) collective-permute-start(f32[13,64,512]{2,1,0:T(8,128)} %get-tuple-element.23), channel_id=1, source_target_pairs={{4,8},{8,4},{12,16},{16,12},{20,24},{24,20},{5,9},{9,5},{13,17},{1... | collective-permute-start | bytes 5111816 | tf_op jit(solution)/shard_map/ppermute | solution.py:541
  6.3 3.7 %copy-start = (f32[16,64,512]{2,1,0:T(8,128)S(1)}, f32[16,64,512]{2,1,0:T(8,128)}, u32[]{:S(2)}) copy-start(f32[16,64,512]{2,1,0:T(8,128)} %level.7) | copy-start | bytes 6291460
  6.3 3.7 %copy-start.1 = (s32[8]{0:T(128)S(1)}, s32[8]{0:T(128)}, u32[]{:S(2)}) copy-start(s32[8]{0:T(128)} %flag.3) | copy-start | bytes 100
  6.3 40.2 %collective-permute-start.1 = (f32[13,64,512]{2,1,0:T(8,128)}, f32[13,64,512]{2,1,0:T(8,128)}, u32[]{:S(2)}, u32[]{:S(2)}) collective-permute-start(f32[13,64,512]{2,1,0:T(8,128)} %get-tuple-element.24), channel_id=1, source_target_pairs={{0,4},{4,0},{8,12},{12,8},{16,20},{20,16},{24,28},{28,24},{1,5},{5... | collective-permute-start | bytes 5111816 | tf_op jit(solution)/shard_map/ppermute | solution.py:542
  12.6 48.0 %all-to-all-start = ((f32[8,96,128]{2,1,0:T(8,128)}), f32[8,96,128]{2,1,0:T(8,128)S(1)}, u32[]{:S(2)}, u32[]{:S(2)}) async-start(f32[8,96,128]{2,1,0:T(8,128)} %first.1), calls=%async_computation | async-start | bytes 786432 | tf_op jit(solution)/shard_map/all_to_all | solution.py:553
  16.4 14.1 %collective-permute-start.2 = (f32[208,512]{1,0:T(8,128)S(1)}, f32[208,512]{1,0:T(8,128)S(1)}, u32[]{:S(2)}, u32[]{:S(2)}) collective-permute-start(f32[208,512]{1,0:T(8,128)S(1)} %get-tuple-element.25), channel_id=1, source_target_pairs={{1,0},{2,1},{3,2},{5,4},{6,5},{7,6},{9,8},{10,9},{11,10},{13,12},{... | collective-permute-start | bytes 1277960 | tf_op jit(solution)/shard_map/ppermute | solution.py:545
  19.8 19.8 %collective-permute-start.3 = (f32[208,512]{1,0:T(8,128)S(1)}, f32[208,512]{1,0:T(8,128)S(1)}, u32[]{:S(2)}, u32[]{:S(2)}) collective-permute-start(f32[208,512]{1,0:T(8,128)S(1)} %get-tuple-element.19.after), channel_id=1, source_target_pairs={{0,1},{1,2},{2,3},{4,5},{5,6},{6,7},{8,9},{9,10},{10,11},{12,13},{... | collective-permute-start | bytes 1277960 | tf_op jit(solution)/shard_map/ppermute | solution.py:544
  39.7 12.0 %collective-permute-start.4 = (f32[13,8,512]{2,1,0:T(8,128)S(1)}, f32[13,8,512]{2,1,0:T(8,128)S(1)}, u32[]{:S(2)}, u32[]{:S(2)}) collective-permute-start(f32[13,8,512]{2,1,0:T(8,128)S(1)} %get-tuple-element.26.after), channel_id=1, source_target_pairs={{4,8},{8,4},{12,16},{16,12},{20,24},{24,20},{5,9},{9,5},{13,17},{1... | collective-permute-start | bytes 638984 | tf_op jit(solution)/shard_map/ppermute | solution.py:549
  40.4 11.3 %collective-permute-start.5 = (f32[13,8,512]{2,1,0:T(8,128)S(1)}, f32[13,8,512]{2,1,0:T(8,128)S(1)}, u32[]{:S(2)}, u32[]{:S(2)}) collective-permute-start(f32[13,8,512]{2,1,0:T(8,128)S(1)} %get-tuple-element.32), channel_id=1, source_target_pairs={{0,4},{4,0},{8,12},{12,8},{16,20},{20,16},{24,28},{28,24},{1,5},{5... | collective-permute-start | bytes 638984 | tf_op jit(solution)/shard_map/ppermute | solution.py:550
  51.8 12.4 %copy-start.2 = (s32[8]{0:T(128)S(1)}, s32[8]{0:T(128)}, u32[]{:S(2)}) copy-start(s32[8]{0:T(128)} %rank.3) | copy-start | bytes 100
  60.5 16.2 %all-to-all-start.1 = ((f32[8,96,128]{2,1,0:T(8,128)}), f32[8,96,128]{2,1,0:T(8,128)S(1)}, u32[]{:S(2)}, u32[]{:S(2)}) async-start(f32[8,96,128]{2,1,0:T(8,128)} %get-tuple-element.33), calls=%async_computation.1 | async-start | bytes 786432 | tf_op jit(solution)/shard_map/all_to_all | solution.py:555

commit v4 on v3

--- a/solution.py
+++ b/solution.py
@@ -12,7 +12,8 @@
 step_size = 0.3
 LANES = 128
 SUB = 8
-EARLY = 3
+EARLY = STEPS
+STAGED = 3
 W = STEPS
 
 VMEM = pl.BlockSpec(memory_space=pltpu.VMEM)
@@ -312,26 +313,32 @@
     layer(src, dst, z, row_tiles, speed)
 
 
-def stage_kernel(level, speeds, f0, f1, vel, arrived):
+def staged_tiles(t, own_tiles):
+    return range(t, own_tiles - t) if t <= STAGED else range(0)
+
+
+def stage_kernel(level, speeds, f0, f1, vel, filled, arrived):
     planes, rows, _ = level.shape
+    own_tiles = rows // SUB
+    fill = pltpu.make_async_copy(level, f0.at[pl.ds(0, planes), pl.ds(0, rows), :], filled)
     streams = [
         pltpu.make_async_copy(speeds.at[:, z], vel.at[:, z], arrived.at[z]) for z in range(planes)
     ]
-    for c in streams[1:-1] + [streams[0], streams[-1]]:
+    for c in [fill] + streams[1:-1] + [streams[0], streams[-1]]:
         c.start()
-
-    def fill(z, c):
-        f0[z, 0:rows] = level[z]
-        return c
-
-    lax.fori_loop(0, planes, fill, 0)
-
-    def arriving(z, c):
-        pltpu.make_async_copy(speeds.at[:, z], vel.at[:, z], arrived.at[z]).wait()
-        own_layer(f0, f1, z, range(1, rows // SUB - 1), vel, None)
-        return c
-
-    lax.fori_loop(1, planes - 1, arriving, 0)
+    fill.wait()
+
+    src, dst = f0, f1
+    for t in range(1, STAGED + 1):
+
+        def own(z, c):
+            if t == 1:
+                pltpu.make_async_copy(speeds.at[:, z], vel.at[:, z], arrived.at[z]).wait()
+            own_layer(src, dst, z, staged_tiles(t, own_tiles), vel, None)
+            return c
+
+        lax.fori_loop(t, planes - t, own, 0)
+        src, dst = dst, src
     streams[0].wait()
     streams[-1].wait()
 
@@ -342,12 +349,12 @@
     return pl.pallas_call(
         stage_kernel,
         out_shape=(near(*ext), near(*ext), near(*vel.shape)),
-        in_specs=[VMEM, FAR],
+        in_specs=[FAR, FAR],
         out_specs=(VMEM,) * 3,
-        scratch_shapes=[pltpu.SemaphoreType.DMA((planes,))],
+        scratch_shapes=[pltpu.SemaphoreType.DMA, pltpu.SemaphoreType.DMA((planes,))],
         compiler_params=params(16),
         name="stage",
-    )(*resident(level), *distant(vel))
+    )(*distant(level, vel))
 
 
 def early_kernel(
@@ -373,7 +380,8 @@
 
     src, dst = f0, f1
     for t in range(1, EARLY + 1):
-        done = (0, own_tiles - 1, own_tiles) if t == 1 else range(own_tiles + 1)
+        ready = staged_tiles(t, own_tiles)
+        done = [i for i in range(own_tiles + (t < STEPS)) if i not in ready]
 
         def own(z, c):
             own_layer(src, dst, z, done, vel, edge)

time: 78.5 us -> 82.3 us (1.048)
  Pallas kernels: 28 us -> 31.9 us
    pallas_call x1, Pallas kernels: 2.97 us -> 7.55 us  [stage(): pl.pallas_call(stage_kernel, out_shape=(near(*ext), near(*ext), near(*vel...]
    pallas_call x1, Pallas kernels: 8.71 us -> 7.53 us  [second(): pl.pallas_call(functools.partial(second_kernel, scale=scale), out_shape=(...]
  transfers between devices with their start and end apart: 8 -> 8, of which waited for: 3 -> 3; matrix products, arithmetic and copies ran while one was open for 0% -> 0% of each run, Pallas kernels for 29% -> 33%
where the time goes in v4:
time: 82.3 us; the launch traced here: 81.9 us
  Pallas kernels  31.9 us (39%)
  waiting for transfers between devices  28.5 us (35%)
  starting transfers between devices  20.8 us (25%)
    all_to_all x1, waiting for transfers between devices, program(): parts2 = lax.all_to_all(packed2, 'depth', 0, 0, tiled=True)  11.1 us
    ppermute x1, waiting for transfers between devices, program(): lo = lax.ppermute(to_up, 'image', up)  9.07 us
    ppermute x1, waiting for transfers between devices, program(): hi = lax.ppermute(to_down, 'image', down)  8.24 us
    pallas_call x1, Pallas kernels, stage(): pl.pallas_call(stage_kernel, out_shape=(near(*ext), near(*ext), near(*vel...  7.55 us
    pallas_call x1, Pallas kernels, second(): pl.pallas_call(functools.partial(second_kernel, scale=scale), out_shape=(...  7.53 us
    pallas_call x1, Pallas kernels, early(): pl.pallas_call(early_kernel, out_shape=(near(*ext), near(*ext), near(*hal...  5.74 us
    all_to_all x1, starting transfers between devices, program(): parts = lax.all_to_all(packed, 'depth', 0, 0, tiled=True)  3.88 us
    pallas_call x1, Pallas kernels, depth_pack(): pl.pallas_call(depth_pack_kernel, out_shape=(shape, shape), in_specs=[FAR...  3.77 us
  transfers between devices with their start and end apart: 8, of which 3 were waited for; matrix products, arithmetic and copies ran while one was open for 0% of the time, Pallas kernels for 33%

profile of v4, /device:TPU:4, one launch (start us, length us, event | category | flops | bytes accessed | tf_op | source)
XLA Modules:
  0.0 81.9 jit_solution(9345052222831682742)
XLA Ops:
  0.6 3.8 %depth_pack.1 = (f32[13,64,512]{2,1,0:T(8,128)}, f32[13,64,512]{2,1,0:T(8,128)}) custom-call(f32[16,64,512]{2,1,0:T(8,128)} %level.7, f32[3,16,64,512]{3,2,1,0:T(8,128)} %vel.3), custom_call_target="tpu_custom_call" | custom-call | tf_op jit(solution)/shard_map/depth_pack/pallas_call | solution.py:76
  4.4 1.9 %collective-permute-start = (f32[13,64,512]{2,1,0:T(8,128)}, f32[13,64,512]{2,1,0:T(8,128)}, u32[]{:S(2)}, u32[]{:S(2)}) collective-permute-start(f32[13,64,512]{2,1,0:T(8,128)} %get-tuple-element.23), channel_id=1, source_target_pairs={{4,8},{8,4},{12,16},{16,12},{20,24},{24,20},{5,9},{9,5},{13,17},{1... | collective-permute-start | bytes 5111816 | tf_op jit(solution)/shard_map/ppermute | solution.py:549
  6.3 1.8 %collective-permute-start.1 = (f32[13,64,512]{2,1,0:T(8,128)}, f32[13,64,512]{2,1,0:T(8,128)}, u32[]{:S(2)}, u32[]{:S(2)}) collective-permute-start(f32[13,64,512]{2,1,0:T(8,128)} %get-tuple-element.24), channel_id=1, source_target_pairs={{0,4},{4,0},{8,12},{12,8},{16,20},{20,16},{24,28},{28,24},{1,5},{5... | collective-permute-start | bytes 5111816 | tf_op jit(solution)/shard_map/ppermute | solution.py:550
  8.1 1.8 %image_pack.1 = (f32[208,512]{1,0:T(8,128)S(1)}, f32[208,512]{1,0:T(8,128)S(1)}) custom-call(f32[16,64,512]{2,1,0:T(8,128)} %level.7, f32[3,16,64,512]{3,2,1,0:T(8,128)} %vel.3), custom_call_target="tpu_custom_call" | custom-call | tf_op jit(solution)/shard_map/image_pack/pallas_call | solution.py:117
  9.9 2.6 %first.1 = f32[8,96,128]{2,1,0:T(8,128)} custom-call(s32[8]{0:T(128)S(1)} %copy-done.1, f32[16,64,512]{2,1,0:T(8,128)S(1)} %copy-done, f32[208,512]{1,0:T(8,128)S(1)} %get-tuple-element.19.after), custom_call_target="tpu_custom_call" | custom-call | tf_op jit(solution)/shard_map/first/pallas_call | solution.py:239
  12.6 3.9 %all-to-all-start = ((f32[8,96,128]{2,1,0:T(8,128)}), f32[8,96,128]{2,1,0:T(8,128)S(1)}, u32[]{:S(2)}, u32[]{:S(2)}) async-start(f32[8,96,128]{2,1,0:T(8,128)} %first.1), calls=%async_computation | async-start | bytes 786432 | tf_op jit(solution)/shard_map/all_to_all | solution.py:561
  16.4 3.3 %collective-permute-start.2 = (f32[208,512]{1,0:T(8,128)S(1)}, f32[208,512]{1,0:T(8,128)S(1)}, u32[]{:S(2)}, u32[]{:S(2)}) collective-permute-start(f32[208,512]{1,0:T(8,128)S(1)} %get-tuple-element.25), channel_id=1, source_target_pairs={{1,0},{2,1},{3,2},{5,4},{6,5},{7,6},{9,8},{10,9},{11,10},{13,12},{... | collective-permute-start | bytes 1277960 | tf_op jit(solution)/shard_map/ppermute | solution.py:553
  19.8 2.5 %collective-permute-start.3 = (f32[208,512]{1,0:T(8,128)S(1)}, f32[208,512]{1,0:T(8,128)S(1)}, u32[]{:S(2)}, u32[]{:S(2)}) collective-permute-start(f32[208,512]{1,0:T(8,128)S(1)} %get-tuple-element.19.after), channel_id=1, source_target_pairs={{0,1},{1,2},{2,3},{4,5},{5,6},{6,7},{8,9},{9,10},{10,11},{12,13},{... | collective-permute-start | bytes 1277960 | tf_op jit(solution)/shard_map/ppermute | solution.py:552
  22.3 8.2 %collective-permute-done.2.hi = f32[208,512]{1,0:T(8,128)S(1)} collective-permute-done((f32[208,512]{1,0:T(8,128)S(1)}, f32[208,512]{1,0:T(8,128)S(1)}, u32[]{:S(2)}, u32[]{:S(2)}) %collective-permute-start.2) | collective-permute-done | bytes 426016 | tf_op jit(solution)/shard_map/ppermute | solution.py:553
  30.5 9.1 %collective-permute-done.3.lo = f32[208,512]{1,0:T(8,128)S(1)} collective-permute-done((f32[208,512]{1,0:T(8,128)S(1)}, f32[208,512]{1,0:T(8,128)S(1)}, u32[]{:S(2)}, u32[]{:S(2)}) %collective-permute-start.3) | collective-permute-done | bytes 426016 | tf_op jit(solution)/shard_map/ppermute | solution.py:552
  39.6 0.1 corner_pack.1
  39.7 0.7 collective-permute-start.4
  40.4 3.0 %collective-permute-start.5 = (f32[13,8,512]{2,1,0:T(8,128)S(1)}, f32[13,8,512]{2,1,0:T(8,128)S(1)}, u32[]{:S(2)}, u32[]{:S(2)}) collective-permute-start(f32[13,8,512]{2,1,0:T(8,128)S(1)} %get-tuple-element.32), channel_id=1, source_target_pairs={{0,4},{4,0},{8,12},{12,8},{16,20},{20,16},{24,28},{28,24},{1,5},{5... | collective-permute-start | bytes 638984 | tf_op jit(solution)/shard_map/ppermute | solution.py:558
  43.5 7.5 %stage.1 = (f32[24,72,512]{2,1,0:T(8,128)S(1)}, f32[24,72,512]{2,1,0:T(8,128)S(1)}, f32[3,16,64,512]{3,2,1,0:T(8,128)S(1)}) custom-call(f32[16,64,512]{2,1,0:T(8,128)} %level.7, f32[3,16,64,512]{3,2,1,0:T(8,128)} %vel.3), custom_call_target="tpu_custom_call" | custom-call | tf_op jit(solution)/shard_map/stage/pallas_call | solution.py:349
  51.0 0.0 collective-permute-done.1.inner
  51.0 5.7 %early.1 = (f32[24,72,512]{2,1,0:T(8,128)S(1)}, f32[24,72,512]{2,1,0:T(8,128)S(1)}, f32[9,64,512]{2,1,0:T(8,128)S(1)}, f32[9,64,512]{2,1,0:T(8,128)S(1)}, f32[3,16,8,512]{3,2,1,0:T(8,128)S(1)}) custom-call(f32[24,72,512]{2,1,0:T(8,128)S(1)} %get-tuple-element.20.f0_in, ...), custom_call_target="tpu_custom_call", output_to_operand_aliasing={{0}: (0, {}), {1}: (1, {})} | custom-call | tf_op jit(solution)/shard_map/early/pallas_call | solution.py:400
  56.8 0.0 collective-permute-done.5.cinner
  56.8 0.0 copy-start.2
  56.8 7.5 %second.1 = (f32[8,96,128]{2,1,0:T(8,128)}, f32[16,64,512]{2,1,0:T(8,128)}, f32[24,72,512]{2,1,0:T(8,128)S(1)}, f32[24,72,512]{2,1,0:T(8,128)S(1)}) custom-call(s32[8]{0:T(128)S(1)} %copy-done.1, f32[24,72,512]{2,1,0:T(8,128)S(1)} %get-tuple-element.27.f0, f32[24,72,512]{2,1,0:T(8,128)S(1)} %get-tuple-element.28.f1, ...), custom_call_target="tpu_custom_call", output_to_operand_aliasing={{2}: (1, {}), {3}: (2, {})} | custom-call | tf_op jit(solution)/shard_map/second/pallas_call | solution.py:476
  64.4 0.0 all-to-all-done.parts
  64.4 3.7 %all-to-all-start.1 = ((f32[8,96,128]{2,1,0:T(8,128)}), f32[8,96,128]{2,1,0:T(8,128)S(1)}, u32[]{:S(2)}, u32[]{:S(2)}) async-start(f32[8,96,128]{2,1,0:T(8,128)} %get-tuple-element.33), calls=%async_computation.1 | async-start | bytes 786432 | tf_op jit(solution)/shard_map/all_to_all | solution.py:563
  68.0 1.4 %composite.2 = f32[4,64,64]{2,1,0:T(8,128)} custom-call(s32[8]{0:T(128)S(1)} %copy-done.2, f32[8,96,128]{2,1,0:T(8,128)S(1)} %all-to-all-done.parts), custom_call_target="tpu_custom_call" | custom-call | tf_op jit(solution)/shard_map/composite/pallas_call | solution.py:526
  69.4 11.1 %all-to-all-done.1.parts = f32[8,96,128]{2,1,0:T(8,128)S(1)} async-done(((f32[8,96,128]{2,1,0:T(8,128)}), f32[8,96,128]{2,1,0:T(8,128)S(1)}, u32[]{:S(2)}, u32[]{:S(2)}) %all-to-all-start.1) | async-done | bytes 393248 | tf_op jit(solution)/shard_map/all_to_all | solution.py:563
  80.6 1.4 %composite.3 = f32[4,64,64]{2,1,0:T(8,128)} custom-call(s32[8]{0:T(128)S(1)} %copy-done.2, f32[8,96,128]{2,1,0:T(8,128)S(1)} %all-to-all-done.1.parts), custom_call_target="tpu_custom_call" | custom-call | tf_op jit(solution)/shard_map/composite/pallas_call | solution.py:526
  (7 shorter events, 0.0 us)
Async XLA Ops:
  4.4 46.6 %collective-permute-start = (f32[13,64,512]{2,1,0:T(8,128)}, f32[13,64,512]{2,1,0:T(8,128)}, u32[]{:S(2)}, u32[]{:S(2)}) collective-permute-start(f32[13,64,512]{2,1,0:T(8,128)} %get-tuple-element.23), channel_id=1, source_target_pairs={{4,8},{8,4},{12,16},{16,12},{20,24},{24,20},{5,9},{9,5},{13,17},{1... | collective-permute-start | bytes 5111816 | tf_op jit(solution)/shard_map/ppermute | solution.py:549
  6.3 3.7 %copy-start = (f32[16,64,512]{2,1,0:T(8,128)S(1)}, f32[16,64,512]{2,1,0:T(8,128)}, u32[]{:S(2)}) copy-start(f32[16,64,512]{2,1,0:T(8,128)} %level.7) | copy-start | bytes 6291460
  6.3 3.7 %copy-start.1 = (s32[8]{0:T(128)S(1)}, s32[8]{0:T(128)}, u32[]{:S(2)}) copy-start(s32[8]{0:T(128)} %flag.3) | copy-start | bytes 100
  6.3 44.8 %collective-permute-start.1 = (f32[13,64,512]{2,1,0:T(8,128)}, f32[13,64,512]{2,1,0:T(8,128)}, u32[]{:S(2)}, u32[]{:S(2)}) collective-permute-start(f32[13,64,512]{2,1,0:T(8,128)} %get-tuple-element.24), channel_id=1, source_target_pairs={{0,4},{4,0},{8,12},{12,8},{16,20},{20,16},{24,28},{28,24},{1,5},{5... | collective-permute-start | bytes 5111816 | tf_op jit(solution)/shard_map/ppermute | solution.py:550
  12.6 51.8 %all-to-all-start = ((f32[8,96,128]{2,1,0:T(8,128)}), f32[8,96,128]{2,1,0:T(8,128)S(1)}, u32[]{:S(2)}, u32[]{:S(2)}) async-start(f32[8,96,128]{2,1,0:T(8,128)} %first.1), calls=%async_computation | async-start | bytes 786432 | tf_op jit(solution)/shard_map/all_to_all | solution.py:561
  16.4 14.1 %collective-permute-start.2 = (f32[208,512]{1,0:T(8,128)S(1)}, f32[208,512]{1,0:T(8,128)S(1)}, u32[]{:S(2)}, u32[]{:S(2)}) collective-permute-start(f32[208,512]{1,0:T(8,128)S(1)} %get-tuple-element.25), channel_id=1, source_target_pairs={{1,0},{2,1},{3,2},{5,4},{6,5},{7,6},{9,8},{10,9},{11,10},{13,12},{... | collective-permute-start | bytes 1277960 | tf_op jit(solution)/shard_map/ppermute | solution.py:553
  19.8 19.8 %collective-permute-start.3 = (f32[208,512]{1,0:T(8,128)S(1)}, f32[208,512]{1,0:T(8,128)S(1)}, u32[]{:S(2)}, u32[]{:S(2)}) collective-permute-start(f32[208,512]{1,0:T(8,128)S(1)} %get-tuple-element.19.after), channel_id=1, source_target_pairs={{0,1},{1,2},{2,3},{4,5},{5,6},{6,7},{8,9},{9,10},{10,11},{12,13},{... | collective-permute-start | bytes 1277960 | tf_op jit(solution)/shard_map/ppermute | solution.py:552
  39.7 17.1 %collective-permute-start.4 = (f32[13,8,512]{2,1,0:T(8,128)S(1)}, f32[13,8,512]{2,1,0:T(8,128)S(1)}, u32[]{:S(2)}, u32[]{:S(2)}) collective-permute-start(f32[13,8,512]{2,1,0:T(8,128)S(1)} %get-tuple-element.26.after), channel_id=1, source_target_pairs={{4,8},{8,4},{12,16},{16,12},{20,24},{24,20},{5,9},{9,5},{13,17},{1... | collective-permute-start | bytes 638984 | tf_op jit(solution)/shard_map/ppermute | solution.py:557
  40.4 16.4 %collective-permute-start.5 = (f32[13,8,512]{2,1,0:T(8,128)S(1)}, f32[13,8,512]{2,1,0:T(8,128)S(1)}, u32[]{:S(2)}, u32[]{:S(2)}) collective-permute-start(f32[13,8,512]{2,1,0:T(8,128)S(1)} %get-tuple-element.32), channel_id=1, source_target_pairs={{0,4},{4,0},{8,12},{12,8},{16,20},{20,16},{24,28},{28,24},{1,5},{5... | collective-permute-start | bytes 638984 | tf_op jit(solution)/shard_map/ppermute | solution.py:558
  56.8 11.2 %copy-start.2 = (s32[8]{0:T(128)S(1)}, s32[8]{0:T(128)}, u32[]{:S(2)}) copy-start(s32[8]{0:T(128)} %rank.3) | copy-start | bytes 100
  64.4 16.2 %all-to-all-start.1 = ((f32[8,96,128]{2,1,0:T(8,128)}), f32[8,96,128]{2,1,0:T(8,128)S(1)}, u32[]{:S(2)}, u32[]{:S(2)}) async-start(f32[8,96,128]{2,1,0:T(8,128)} %get-tuple-element.33), calls=%async_computation.1 | async-start | bytes 786432 | tf_op jit(solution)/shard_map/all_to_all | solution.py:563
